TPU v7x, 128 devices: a whole 4x4x4 slice. The times are simulated.
128 devices in a mesh: gx: 4 (over y), gy: 4 (over z_hi, core), gz: 8 (over z_lo, x).
Axes of the slice: x: 4, y: 4, z: 4 (z_hi: 2, z_lo: 2; z = z_hi * 2 + z_lo), core: 2. Of those that a mesh axis runs over, the one named last changes fastest.
Arguments:
- volume: bfloat16 [32, 32, 32, 32, 128], P('gx', 'gy', 'gz'), may hold values from -6 to 6
- conv_kernel: bfloat16 [3, 3, 3, 32, 64], replicated, may hold values from -0.21875 to 0.21875
- dense_one: bfloat16 [16, 16, 16, 64, 2048], P('gx', None, None, ('gy', 'gz')), may hold values from -0.01171875 to 0.01171875
- dense_two: float32 [2048, 256], replicated, may hold values from -0.125 to 0.125
- dense_three: float32 [256, 4], replicated, may hold values from -0.375 to 0.375
- targets: float32 [4, 128], replicated, may hold values from -3 to 3
Outputs:
- prediction: float32 [4, 128], replicated
- grad_dense_one: bfloat16 [16, 16, 16, 64, 2048], P('gx', None, None, ('gy', 'gz'))
- grad_conv: float32 [3, 3, 3, 32, 64], replicated
- grad_volume: bfloat16 [32, 32, 32, 32, 128], P('gx', 'gy', 'gz')
All inputs are finite; a program needn't handle non-finite values.
Results may differ from a plain program's by a relative error of at most 0.008.
Values may be sent and summed in bfloat16 or wider, within the bound.
No kernel may reach another device: no remote copies, remote signals or barrier semaphores. Data moves between devices by JAX's collectives and lax.ppermute only.
A program may use at most 128 MiB of HBM per device.

v0:
```python
import jax
import jax.numpy as jnp
from jax import lax
from jax.experimental import pallas as pl
from jax.experimental.pallas import tpu as pltpu
from jax.sharding import PartitionSpec as P

loss_scale = 1024.0
leak_slope = 0.3
everyone = ("gx", "gy", "gz")
bf16 = jnp.bfloat16
f32 = jnp.float32


def in_hbm(array):
    return pltpu.with_memory_space_constraint(array, pltpu.HBM)


def neighbours(axis):
    size = lax.axis_size(axis)
    up = [(i, i + 1) for i in range(size - 1)]
    return up, [(j, i) for i, j in up]


def both_ways(toward_up, toward_down, axis):
    up, down = neighbours(axis)
    return lax.ppermute(toward_up, axis, up), lax.ppermute(toward_down, axis, down)


def smooth_leaky(values):
    return leak_slope * values + (1.0 - leak_slope) * jax.nn.softplus(values)


def leaky_derivative(values):
    return leak_slope + (1.0 - leak_slope) * jax.nn.sigmoid(values)


def banded_kernel(kernel, cells):
    taps_x, taps_y, _, c_in, c_out = kernel.shape
    bands = [
        jnp.pad(kernel, ((0, 0), (0, 0), (z, cells - 1 - z), (0, 0), (0, 0)))
        for z in range(cells)
    ]
    whole = jnp.stack(bands)
    return jnp.transpose(whole, (3, 4, 1, 2, 0, 5)).reshape(
        (cells + 2) * c_in, taps_x * taps_y * cells * c_out
    )


def forward_call(core, x_lo, x_hi, y_lo, y_hi, z_lo, z_hi, twice):
    nx, ny, width, lanes = core.shape
    edge = z_lo.shape[2]
    depth = width + 2 * edge
    half = twice.shape[1] // 2
    rows = 4 * half
    tap = 3 * edge

    def build(twice, matrix):
        for pair in range(2):
            for start in range(0, 9, 2):
                count = min(2, 9 - start)
                side = lax.broadcasted_iota(jnp.int32, (tap, 2 * half), 1) < half
                blocks = []
                for k in range(start, start + count):
                    block = twice[k * tap : (k + 1) * tap, :]
                    blocks.append(jnp.where(side, block, jnp.zeros_like(block)))
                    blocks.append(jnp.where(side, jnp.zeros_like(block), block))
                stacked = jnp.concatenate(blocks, axis=0)
                size = count * depth
                here = lax.broadcasted_iota(jnp.int32, (size, size), 0)
                from_row = lax.broadcasted_iota(jnp.int32, (size, size), 1)
                which = from_row // tap
                moved = (
                    (which // 2) * depth + (2 * pair + which % 2) * edge + from_row - which * tap
                )
                place = jnp.where(here == moved, 1.0, 0.0).astype(bf16)
                matrix[
                    pair * 2 * half : (pair + 1) * 2 * half,
                    start * depth : (start + count) * depth,
                ] = lax.dot_general(
                    stacked, place, (((0,), (1,)), ((), ())), preferred_element_type=f32
                ).astype(bf16)

    def body(
        core, x_lo, x_hi, y_lo, y_hi, z_lo, z_hi, twice, kept, conv_out, pooled, padded, matrix, sem
    ):
        step = pl.program_id(0)

        @pl.when(step == 0)
        def _():
            middle = pl.ds(edge, width)
            padded[1 : nx + 1, 1 : ny + 1, middle, :] = core[...]
            padded[0, 1 : ny + 1, middle, :] = x_lo[...]
            padded[nx + 1, 1 : ny + 1, middle, :] = x_hi[...]
            padded[:, 0, middle, :] = y_lo[...]
            padded[:, ny + 1, middle, :] = y_hi[...]
            padded[:, :, 0:edge, :] = z_lo[...]
            padded[:, :, edge + width : depth, :] = z_hi[...]
            pltpu.make_async_copy(padded, kept, sem).start()
            build(twice, matrix)

        weights = matrix[...]
        for pair in range(ny // 2):
            y = 2 * pair
            total = None
            for inner in range(2):
                x = 2 * step + inner
                patch = jnp.concatenate(
                    [
                        jnp.concatenate(
                            [padded[x + dx, y + dy], padded[x + dx, y + dy + 1]], axis=1
                        )
                        for dx in range(3)
                        for dy in range(3)
                    ],
                    axis=0,
                )
                values = jnp.dot(weights, patch, preferred_element_type=f32)
                conv_out[inner, y] = values[:, :lanes].astype(bf16)
                conv_out[inner, y + 1] = values[:, lanes:].astype(bf16)
                soft = jnp.maximum(values, 0.0) + jnp.log(1.0 + jnp.exp(-jnp.abs(values)))
                acted = leak_slope * values + (1.0 - leak_slope) * soft
                across = acted[:, :lanes] + acted[:, lanes:]
                total = across if total is None else total + across
            total = total * 0.125
            pooled[0, pair, 0] = (total[:half] + total[half : 2 * half]).astype(bf16)
            pooled[0, pair, 1] = (total[2 * half : 3 * half] + total[3 * half :]).astype(bf16)

        @pl.when(step == nx // 2 - 1)
        def _():
            pltpu.make_async_copy(padded, kept, sem).wait()

    def whole(array):
        return pl.BlockSpec(array.shape, lambda i: (0,) * array.ndim)

    operands = (in_hbm(core), x_lo, x_hi, y_lo, y_hi, z_lo, z_hi, twice)
    padded_shape = (nx + 2, ny + 2, depth, lanes)
    return pl.pallas_call(
        body,
        grid=(nx // 2,),
        in_specs=[whole(a) for a in operands],
        out_specs=[
            pl.BlockSpec(memory_space=pltpu.HBM),
            pl.BlockSpec((2, ny, rows, lanes), lambda i: (i, 0, 0, 0)),
            pl.BlockSpec((1, ny // 2, 2, half, lanes), lambda i: (i, 0, 0, 0, 0)),
        ],
        out_shape=[
            pltpu.HBM(padded_shape, bf16),
            pltpu.HBM((nx, ny, rows, lanes), bf16),
            jax.ShapeDtypeStruct((nx // 2, ny // 2, 2, half, lanes), bf16),
        ],
        scratch_shapes=[
            pltpu.VMEM(padded_shape, bf16),
            pltpu.VMEM((rows, 9 * depth), bf16),
            pltpu.SemaphoreType.DMA,
        ],
        compiler_params=pltpu.CompilerParams(vmem_limit_bytes=40 * 2**20),
        cost_estimate=pl.CostEstimate(flops=7 * 10**9, bytes_accessed=16 * 2**20, transcendentals=0),
        name="conv_forward",
    )(*operands)


def kernel_grad_call(padded, conv_out, grad_pooled, c_in):
    nx, ny, rows, lanes = conv_out.shape
    depth = padded.shape[2]
    c_out = rows // 4

    def body(rows_0, rows_1, conv_out, grad_pooled, grad_out, result, sums):
        step = pl.program_id(0)

        @pl.when(step == 0)
        def _():
            sums[...] = jnp.zeros(sums.shape, f32)

        for x in range(2):
            for y in range(ny):
                values = conv_out[x, y].astype(f32)
                rise = (1.0 - leak_slope) / 16.0
                slope = (leak_slope / 8.0 + rise) + rise * jnp.tanh(0.5 * values)
                pieces = [grad_pooled[0, y // 2, z // 2].astype(f32) for z in range(4)]
                grad_out[x, y] = (jnp.concatenate(pieces, axis=0) * slope).astype(bf16)
        layers = [rows_0.at[0], rows_0.at[1], rows_1.at[0], rows_1.at[1]]
        right = jnp.concatenate(
            [grad_out[x, y] for x in range(2) for y in range(ny)], axis=1
        )
        for dx in range(3):
            left = jnp.concatenate(
                [
                    jnp.concatenate(
                        [layers[x + dx][y + dy] for x in range(2) for y in range(ny)], axis=1
                    )
                    for dy in range(3)
                ],
                axis=0,
            )
            sums[dx] += lax.dot_general(
                left, right, (((1,), (1,)), ((), ())), preferred_element_type=f32
            )

        @pl.when(step == nx // 2 - 1)
        def _():
            for dx in range(3):
                for dy in range(3):
                    for dz in range(3):
                        total = None
                        for z in range(4):
                            start = dy * depth + (z + dz) * c_in
                            piece = sums[dx, start : start + c_in, z * c_out : (z + 1) * c_out]
                            total = piece if total is None else total + piece
                        result[9 * dx + 3 * dy + dz] = total

    return pl.pallas_call(
        body,
        grid=(nx // 2,),
        in_specs=[
            pl.BlockSpec((2,) + padded.shape[1:], lambda i: (i, 0, 0, 0)),
            pl.BlockSpec((2,) + padded.shape[1:], lambda i: (i + 1, 0, 0, 0)),
            pl.BlockSpec((2, ny, rows, lanes), lambda i: (i, 0, 0, 0)),
            pl.BlockSpec((1,) + grad_pooled.shape[1:], lambda i: (i, 0, 0, 0, 0)),
        ],
        out_specs=[
            pl.BlockSpec((2, ny, rows, lanes), lambda i: (i, 0, 0, 0)),
            pl.BlockSpec((27, c_in, c_out), lambda i: (0, 0, 0)),
        ],
        out_shape=[
            pltpu.HBM((nx, ny, rows, lanes), bf16),
            jax.ShapeDtypeStruct((27, c_in, c_out), f32),
        ],
        scratch_shapes=[pltpu.VMEM((3, 3 * depth, rows), f32)],
        compiler_params=pltpu.CompilerParams(vmem_limit_bytes=32 * 2**20),
        cost_estimate=pl.CostEstimate(flops=8 * 10**9, bytes_accessed=14 * 2**20, transcendentals=0),
        name="conv_kernel_grad",
    )(in_hbm(padded), in_hbm(padded), in_hbm(conv_out), grad_pooled)


def input_grad_call(grad_out, matrix):
    nx, ny, rows, lanes = grad_out.shape
    depth = matrix.shape[0]

    def body(grad_out, matrix, spread, held):
        step = pl.program_id(0)

        @pl.when(step == 0)
        def _():
            for edge in (0, nx + 2):
                held[edge : edge + 2] = jnp.zeros((2,) + held.shape[1:], bf16)
            for edge in (0, ny + 2):
                held[2 : nx + 2, edge : edge + 2] = jnp.zeros((nx, 2, rows, lanes), bf16)

        @pl.when(step < nx // 2)
        def _():
            held[pl.ds(2 * step + 2, 2), 2 : ny + 2] = grad_out[...]

        for x in range(2):
            at = 2 * step + 2 + x
            for pair in range((ny + 2) // 2):
                y = 2 * pair
                taps = [dy for dy in range(3) if y + 1 - dy >= 0 and y - dy < ny]
                values = None
                for dx in range(3):
                    patch = jnp.concatenate(
                        [
                            jnp.concatenate(
                                [held[at - dx, y + 2 - dy], held[at - dx, y + 3 - dy]], axis=1
                            )
                            for dy in taps
                        ],
                        axis=0,
                    )
                    start = (3 * dx + taps[0]) * rows
                    term = jnp.dot(
                        matrix[:, start : start + len(taps) * rows],
                        patch,
                        preferred_element_type=f32,
                    )
                    values = term if values is None else values + term
                values = values.astype(bf16)
                spread[x, y] = values[:, :lanes]
                spread[x, y + 1] = values[:, lanes:]

    return pl.pallas_call(
        body,
        grid=(nx // 2 + 1,),
        in_specs=[
            pl.BlockSpec((2, ny, rows, lanes), lambda i: (jnp.minimum(i, nx // 2 - 1), 0, 0, 0)),
            pl.BlockSpec(matrix.shape, lambda i: (0, 0)),
        ],
        out_specs=pl.BlockSpec((2, ny + 2, depth, lanes), lambda i: (i, 0, 0, 0)),
        out_shape=pltpu.HBM((nx + 2, ny + 2, depth, lanes), bf16),
        scratch_shapes=[pltpu.VMEM((nx + 4, ny + 4, rows, lanes), bf16)],
        compiler_params=pltpu.CompilerParams(vmem_limit_bytes=40 * 2**20),
        cost_estimate=pl.CostEstimate(flops=9 * 10**9, bytes_accessed=12 * 2**20, transcendentals=0),
        name="conv_input_grad",
    )(in_hbm(grad_out), matrix)


def finish_call(spread, x_lo, x_hi, y_lo, y_hi, z_lo, z_hi):
    nx, ny, edge, lanes = z_lo.shape
    depth = spread.shape[2]
    width = depth - 2 * edge

    def body(spread_0, spread_1, x_lo, x_hi, y_lo, y_hi, z_lo, z_hi, result):
        step = pl.program_id(0)
        middle = slice(edge, edge + width)

        def base(x, y):
            value = (spread_0, spread_1)[x][0, y + 1, middle].astype(f32)
            if y == 0:
                value = value + y_lo[x, middle].astype(f32)
            if y == ny - 1:
                value = value + y_hi[x, middle].astype(f32)
            low = value[:edge] + z_lo[x, y].astype(f32)
            high = value[width - edge :] + z_hi[x, y].astype(f32)
            return jnp.concatenate([low, value[edge : width - edge], high], axis=0)

        def write(x, term):
            for y in range(ny):
                value = base(x, y)
                if term is not None:
                    value = value + term[y + 1, middle].astype(f32)
                result[x, y] = value.astype(bf16)

        @pl.when(step == 0)
        def _():
            write(0, x_lo)

        @pl.when(step > 0)
        def _():
            write(0, None)

        @pl.when(step == nx // 2 - 1)
        def _():
            write(1, x_hi)

        @pl.when(step < nx // 2 - 1)
        def _():
            write(1, None)

    def whole(array):
        return pl.BlockSpec(array.shape, lambda i: (0,) * array.ndim)

    def sliced(array):
        return pl.BlockSpec((2,) + array.shape[1:], lambda i: (i,) + (0,) * (array.ndim - 1))

    return pl.pallas_call(
        body,
        grid=(nx // 2,),
        in_specs=[
            pl.BlockSpec((1,) + spread.shape[1:], lambda i: (2 * i + 1, 0, 0, 0)),
            pl.BlockSpec((1,) + spread.shape[1:], lambda i: (2 * i + 2, 0, 0, 0)),
            whole(x_lo),
            whole(x_hi),
            sliced(y_lo),
            sliced(y_hi),
            sliced(z_lo),
            sliced(z_hi),
        ],
        out_specs=pl.BlockSpec((2, ny, width, lanes), lambda i: (i, 0, 0, 0)),
        out_shape=jax.ShapeDtypeStruct((nx, ny, width, lanes), bf16),
        compiler_params=pltpu.CompilerParams(vmem_limit_bytes=24 * 2**20),
        cost_estimate=pl.CostEstimate(flops=10**8, bytes_accessed=10 * 2**20, transcendentals=0),
        name="fold_faces",
    )(
        in_hbm(spread),
        in_hbm(spread),
        x_lo,
        x_hi,
        in_hbm(y_lo),
        in_hbm(y_hi),
        in_hbm(z_lo),
        in_hbm(z_hi),
    )


def exchange(array, axes):
    return lax.all_to_all(array, axes, split_axis=0, concat_axis=0, tiled=True)


def body(volume, conv_kernel, dense_one, dense_two, dense_three, targets):
    nx, ny, nz, c_in, samples = volume.shape
    c_out = conv_kernel.shape[4]
    groups_y = lax.axis_size("gy")
    groups_z = lax.axis_size("gz")
    groups = groups_y * groups_z
    devices = lax.axis_size(everyone)
    per_group = c_out // groups

    core = volume.reshape(nx, ny, nz * c_in, samples)
    x_lo, x_hi = both_ways(core[-1:], core[:1], "gx")
    first = jnp.concatenate([x_lo[:, :1], core[:, :1], x_hi[:, :1]], axis=0)
    last = jnp.concatenate([x_lo[:, -1:], core[:, -1:], x_hi[:, -1:]], axis=0)
    y_lo, y_hi = both_ways(last, first, "gy")

    def z_layer(rows):
        sides = [a[:, :, rows] for a in (y_lo, x_lo, core, x_hi, y_hi)]
        middle = jnp.concatenate(sides[1:4], axis=0)
        return jnp.concatenate([sides[0], middle, sides[4]], axis=1)

    z_lo, z_hi = both_ways(z_layer(slice(-c_in, None)), z_layer(slice(0, c_in)), "gz")
    backward_matrix = banded_kernel(conv_kernel, nz)
    twice = conv_kernel.reshape(-1, c_out)
    twice = jnp.concatenate([twice, twice], axis=1)
    padded, conv_out, pooled = forward_call(
        core, x_lo[0], x_hi[0], y_lo[:, 0], y_hi[:, 0], z_lo, z_hi, twice
    )

    half_x, half_y, half_z = nx // 2, ny // 2, nz // 2
    cells = half_x * half_y * half_z
    outgoing = pooled.reshape(cells, groups, per_group, samples).transpose(1, 0, 2, 3)
    arrived = exchange(outgoing.reshape(groups, cells * per_group, samples), ("gy", "gz"))
    arrived = arrived.reshape(groups_y, groups_z, half_x, half_y, half_z, per_group, samples)
    features = arrived.transpose(2, 0, 3, 1, 4, 5, 6).reshape(-1, samples)
    weights = lax.optimization_barrier(dense_one.reshape(-1, dense_one.shape[4]))
    partial_one = lax.dot_general(
        features, weights, (((0,), (0,)), ((), ())), preferred_element_type=f32
    )
    rows = partial_one.shape[1] // 128
    gathered = exchange(partial_one.astype(bf16).reshape(devices, rows, 128), everyone)
    pre_one = gathered.astype(f32).sum(axis=0).reshape(1, rows * 128)
    mine = lax.axis_index(everyone)
    target = lax.dynamic_slice_in_dim(targets, mine, 1, axis=1).T
    hidden_one = smooth_leaky(pre_one)
    pre_two = jnp.dot(hidden_one, dense_two, precision=lax.Precision.HIGHEST)
    hidden_two = smooth_leaky(pre_two)
    own_prediction = jnp.dot(hidden_two, dense_three, precision=lax.Precision.HIGHEST)
    error_grad = loss_scale * (own_prediction - target)
    grad_pre_two = jnp.dot(
        error_grad, dense_three.T, precision=lax.Precision.HIGHEST
    ) * leaky_derivative(pre_two)
    own_grad = (
        jnp.dot(grad_pre_two, dense_two.T, precision=lax.Precision.HIGHEST)
        * leaky_derivative(pre_one)
    ).astype(bf16)
    copies = jnp.broadcast_to(own_grad.reshape(1, rows, 128), (devices, rows, 128))
    grad_pre_one = exchange(copies, everyone).reshape(samples, rows * 128)

    grad_features = lax.dot_general(
        weights, grad_pre_one, (((1,), (1,)), ((), ())), preferred_element_type=f32
    ).astype(bf16)
    grad_features = grad_features.reshape(
        half_x, groups_y, half_y, groups_z, half_z, per_group, samples
    ).transpose(1, 3, 0, 2, 4, 5, 6)
    returned = exchange(grad_features.reshape(groups, cells * per_group, samples), ("gy", "gz"))
    grad_dense_one = (
        jnp.einsum("uvxyzcb,bh->xuyvzch", arrived, grad_pre_one, preferred_element_type=f32)
        / samples
    ).astype(bf16).reshape(dense_one.shape)
    grad_pooled = (
        returned.reshape(groups, cells, per_group, samples).transpose(1, 0, 2, 3)
    ).reshape(pooled.shape)

    grad_out, kernel_local = kernel_grad_call(padded, conv_out, grad_pooled, c_in)
    spread = input_grad_call(grad_out, backward_matrix)
    from_lo, from_hi = both_ways(spread[-1], spread[0], "gx")

    def added(array, first_term, last_term):
        head = (array[:1].astype(f32) + first_term.astype(f32)).astype(bf16)
        tail = (array[-1:].astype(f32) + last_term.astype(f32)).astype(bf16)
        return jnp.concatenate([head, array[1:-1], tail], axis=0)

    y_down = added(spread[1:-1, 0], from_lo[None, 0], from_hi[None, 0])
    y_up = added(spread[1:-1, -1], from_lo[None, -1], from_hi[None, -1])
    y_lo_terms, y_hi_terms = both_ways(y_up, y_down, "gy")

    def with_edges(part):
        face = spread[1:-1, 1:-1, part]
        face = added(face, from_lo[None, 1:-1, part], from_hi[None, 1:-1, part])
        head = (face[:, :1].astype(f32) + y_lo_terms[:, None, part].astype(f32)).astype(bf16)
        tail = (face[:, -1:].astype(f32) + y_hi_terms[:, None, part].astype(f32)).astype(bf16)
        return jnp.concatenate([head, face[:, 1:-1], tail], axis=1)

    z_down = with_edges(slice(0, c_in))
    z_up = with_edges(slice(-c_in, None))
    z_lo_terms, z_hi_terms = both_ways(z_up, z_down, "gz")
    grad_volume = finish_call(
        spread, from_lo, from_hi, y_lo_terms, y_hi_terms, z_lo_terms, z_hi_terms
    ).reshape(volume.shape)

    share = kernel_local.size // devices
    pieces = jnp.pad(kernel_local.reshape(devices, share), ((0, 0), (0, 512 - share)))
    pieces = exchange(pieces.reshape(devices, 4, 128), everyone)
    own_piece = (pieces.sum(axis=0) / samples).reshape(512)
    own_piece = jnp.concatenate(
        [own_piece[:share], own_prediction.reshape(-1), jnp.zeros((508 - share,), f32)]
    )
    results = exchange(
        jnp.broadcast_to(own_piece.reshape(1, 4, 128), (devices, 4, 128)), everyone
    ).reshape(devices, 512)
    grad_conv = results[:, :share].reshape(conv_kernel.shape)
    prediction = results[:, share : share + 4].T
    return (prediction, grad_dense_one, grad_conv, grad_volume)


def solution(mesh):
    return jax.shard_map(
        body,
        mesh=mesh,
        in_specs=(
            P("gx", "gy", "gz", None, None),
            P(),
            P("gx", None, None, ("gy", "gz"), None),
            P(),
            P(),
            P(),
        ),
        out_specs=(
            P(),
            P("gx", None, None, ("gy", "gz"), None),
            P(),
            P("gx", "gy", "gz", None, None),
        ),
        check_vma=False,
    )
```

profile of v0, /device:TPU:1, one launch (start us, length us, event | category | flops | bytes accessed | tf_op | source)
XLA Modules:
  0.0 255.1 jit_solution(2058012063186768903)
XLA Ops:
  1.9 4.0 %collective-permute-start = (bf16[1,8,128,128]{3,2,1,0:T(8,128)(2,1)S(1)}, bf16[1,8,128,128]{3,2,1,0:T(8,128)(2,1)S(1)}, u32[]{:S(2)}, u32[]{:S(2)}) collective-permute-start(bf16[1,8,128,128]{3,2,1,0:T(8,128)(2,1)S(1)} %bitcast.235), channel_id=1, source_target_pairs={{0,32},{32,64},{64,96},{1,33},{33,65},{65,97},{2,34},{34,66},{66,9... | collective-permute-start | bytes 786440 | tf_op jit(solution)/shard_map/ppermute | solution.py:27
  10.9 3.8 %collective-permute-done.1 = bf16[1,8,128,128]{3,2,1,0:T(8,128)(2,1)S(1)} collective-permute-done((bf16[1,8,128,128]{3,2,1,0:T(8,128)(2,1)S(1)}, bf16[1,8,128,128]{3,2,1,0:T(8,128)(2,1)S(1)}, u32[]{:S(2)}, u32[]{:S(2)}) %collective-permute-start.1) | collective-permute-done | bytes 262176 | tf_op jit(solution)/shard_map/ppermute | solution.py:27
  18.6 5.4 %collective-permute-start.2 = (bf16[10,1,128,128]{3,2,1,0:T(8,128)(2,1)S(1)}, bf16[10,1,128,128]{3,2,1,0:T(8,128)(2,1)S(1)}, u32[]{:S(2)}, u32[]{:S(2)}) collective-permute-start(bf16[10,1,128,128]{3,2,1,0:T(8,128)(2,1)S(1)} %pad_maximum_fusion.8), channel_id=1, source_target_pairs={{0,8},{8,16},{16,24},{1,9},{9,17},{17,25},{2,10},{10,18},{18,26},{... | collective-permute-start | bytes 983048 | tf_op jit(solution)/shard_map/ppermute | solution.py:27
  29.6 4.0 %collective-permute-start.4 = (bf16[10,10,32,128]{3,2,1,0:T(8,128)(2,1)S(1)}, bf16[10,10,32,128]{3,2,1,0:T(8,128)(2,1)S(1)}, u32[]{:S(2)}, u32[]{:S(2)}) collective-permute-start(bf16[10,10,32,128]{3,2,1,0:T(8,128)(2,1)S(1)} %pad_maximum_fusion), channel_id=1, source_target_pairs={{0,1},{1,2},{2,3},{3,4},{4,5},{5,6},{6,7},{8,9},{9,10},{10,11},{11... | collective-permute-start | bytes 2457608 | tf_op jit(solution)/shard_map/ppermute | solution.py:27
  33.8 10.9 %collective-permute-done.5.z_hi = bf16[10,10,32,128]{3,2,1,0:T(8,128)(2,1)S(1)} collective-permute-done((bf16[10,10,32,128]{3,2,1,0:T(8,128)(2,1)S(1)}, bf16[10,10,32,128]{3,2,1,0:T(8,128)(2,1)S(1)}, u32[]{:S(2)}, u32[]{:S(2)}) %collective-permute-start.5) | collective-permute-done | bytes 819232 | tf_op jit(solution)/shard_map/ppermute | solution.py:27
  46.6 14.4 %conv_forward.1 = (bf16[10,10,192,128]{3,2,1,0:T(8,128)(2,1)}, bf16[8,8,256,128]{3,2,1,0:T(8,128)(2,1)}, bf16[4,4,2,64,128]{4,3,2,1,0:T(8,128)(2,1)S(1)}) custom-call(bf16[8,8,128,128]{3,2,1,0:T(8,128)(2,1)} %bitcast.223, bf16[8,128,128]{2,1,0:T(8,128)(2,1)S(1)} %bitcast.213, bf16[8,128,128]{2,1,0:T(8,128)(2,1)S(1)} %bitcast.214, ...), custom_call_target="tpu_custom_call" | custom-call | flops 7000000000 | bytes 16777216 | tf_op jit(solution)/shard_map/conv_forward/pallas_call | solution.py:138
  62.1 10.2 %all-to-all-start = ((bf16[32,64,128]{2,1,0:T(8,128)(2,1)}), bf16[32,64,128]{2,1,0:T(8,128)(2,1)S(1)}, u32[]{:S(2)}, u32[]{:S(2)}) async-start(bf16[32,64,128]{2,1,0:T(8,128)(2,1)} %copy.46), calls=%async_computation | async-start | bytes 1048576 | tf_op jit(solution)/shard_map/all_to_all | solution.py:376
  72.3 13.1 %reshape.235 = bf16[2048,2048]{1,0:T(8,128)(2,1)} reshape(bf16[4,16,16,2,2048]{4,3,2,1,0:T(2,128)(2,1)} %param.8) | data formatting | bytes 16777216 | tf_op jit(solution)/shard_map/reshape | solution.py:413
  86.5 4.7 %fusion.2 = bf16[16,8,16,128]{3,1,2,0:T(8,128)(2,1)S(1)} fusion(bf16[2048,128]{1,0:T(8,128)(2,1)S(1)} %bitcast.219, bf16[2048,2048]{1,0:T(8,128)(2,1)} %reshape.235), kind=kOutput, calls=%fused_computation.6 | convolution fusion | flops 1074003968 | bytes 9437184 | tf_op jit(solution)/shard_map/dot_general | solution.py:414
  92.1 9.1 %all-to-all-start.1 = ((bf16[128,16,128]{2,1,0:T(8,128)(2,1)}), bf16[128,16,128]{2,1,0:T(8,128)(2,1)S(1)}, u32[]{:S(2)}, u32[]{:S(2)}) async-start(bf16[128,16,128]{2,1,0:T(8,128)(2,1)} %bitcast.87), calls=%async_computation.1 | async-start | bytes 1048576 | tf_op jit(solution)/shard_map/all_to_all | solution.py:376
  101.5 13.8 %all-to-all-done.1 = bf16[128,16,128]{2,1,0:T(8,128)(2,1)S(1)} async-done(((bf16[128,16,128]{2,1,0:T(8,128)(2,1)}), bf16[128,16,128]{2,1,0:T(8,128)(2,1)S(1)}, u32[]{:S(2)}, u32[]{:S(2)}) %all-to-all-start.1) | async-done | bytes 524320 | tf_op jit(solution)/shard_map/all_to_all | solution.py:376
  118.6 17.9 %all_to_all.30 = bf16[128,16,128]{2,1,0:T(8,128)(2,1)S(1)} all-to-all(bf16[128,16,128]{2,1,0:T(8,128)(2,1)S(1)} %broadcast_in_dim.11), channel_id=1, replica_groups=mesh['gx'=4,'gy'=4,'gz'=8] {'gx','gy','gz'}, dimensions={0} | all-to-all | bytes 1048576 | tf_op jit(solution)/shard_map/all_to_all | solution.py:376
  136.5 6.3 %fusion.1 = bf16[2048,128]{0,1:T(8,128)(2,1)S(1)} fusion(bf16[2048,2048]{1,0:T(8,128)(2,1)} %reshape.235, bf16[16,8,16,128]{3,2,1,0:T(8,128)(2,1)S(1)} %bitcast.218), kind=kOutput, calls=%fused_computation.4 | convolution fusion | flops 1074003968 | bytes 9437184 | tf_op jit(solution)/shard_map/dot_general | solution.py:437
  144.2 4.4 %all-to-all-start.3 = ((bf16[32,64,128]{2,1,0:T(8,128)(2,1)}), bf16[32,64,128]{2,1,0:T(8,128)(2,1)S(1)}, u32[]{:S(2)}, u32[]{:S(2)}) async-start(bf16[32,64,128]{2,1,0:T(8,128)(2,1)} %copy.51), calls=%async_computation.3 | async-start | bytes 1048576 | tf_op jit(solution)/shard_map/all_to_all | solution.py:376
  156.0 4.2 %all-to-all-done.3 = bf16[32,64,128]{2,1,0:T(8,128)(2,1)S(1)} async-done(((bf16[32,64,128]{2,1,0:T(8,128)(2,1)}), bf16[32,64,128]{2,1,0:T(8,128)(2,1)S(1)}, u32[]{:S(2)}, u32[]{:S(2)}) %all-to-all-start.3) | async-done | bytes 524320 | tf_op jit(solution)/shard_map/all_to_all | solution.py:376
  161.1 12.1 %conv_kernel_grad.1 = (bf16[8,8,256,128]{3,2,1,0:T(8,128)(2,1)}, f32[27,32,64]{2,1,0:T(8,128)S(1)}) custom-call(bf16[10,10,192,128]{3,2,1,0:T(8,128)(2,1)} %get-tuple-element.9.rows_0.rows_1, bf16[10,10,192,128]{3,2,1,0:T(8,128)(2,1)} %get-tuple-element.9.rows_0.rows_1, bf16[8,8,256,128]{3,2,1,0:T(8,128)(2,1)} %get-tuple-element.10.conv_out, ...), custom_call_target="tpu_custom_call" | custom-call | flops 8000000000 | bytes 14680064 | tf_op jit(solution)/shard_map/conv_kernel_grad/pallas_call | solution.py:212
  173.2 14.1 %conv_input_grad.1.spread_0.spread_1 = bf16[10,10,192,128]{3,2,1,0:T(8,128)(2,1)} custom-call(bf16[8,8,256,128]{3,2,1,0:T(8,128)(2,1)} %get-tuple-element.13.grad_out, bf16[192,2304]{1,0:T(8,128)(2,1)S(1)} %reshape.248.matrix), custom_call_target="tpu_custom_call" | custom-call | flops 8999999488 | bytes 12582912 | tf_op jit(solution)/shard_map/conv_input_grad/pallas_call | solution.py:281
  190.5 3.8 %all-to-all-start.4 = ((f32[128,4,128]{2,1,0:T(4,128)}), f32[128,4,128]{2,1,0:T(4,128)S(1)}, u32[]{:S(2)}, u32[]{:S(2)}) async-start(f32[128,4,128]{2,1,0:T(4,128)} %reshape.244), calls=%async_computation.4 | async-start | bytes 524288 | tf_op jit(solution)/shard_map/all_to_all | solution.py:376
  201.3 4.4 %all-to-all-done.4 = f32[128,4,128]{2,1,0:T(4,128)S(1)} async-done(((f32[128,4,128]{2,1,0:T(4,128)}), f32[128,4,128]{2,1,0:T(4,128)S(1)}, u32[]{:S(2)}, u32[]{:S(2)}) %all-to-all-start.4) | async-done | bytes 262176 | tf_op jit(solution)/shard_map/all_to_all | solution.py:376
  206.7 6.7 %all-to-all-start.5 = ((f32[128,4,128]{2,1,0:T(4,128)}), f32[128,4,128]{2,1,0:T(4,128)S(1)}, u32[]{:S(2)}, u32[]{:S(2)}) async-start(f32[128,4,128]{2,1,0:T(4,128)} %broadcast_in_dim.14), calls=%async_computation.5 | async-start | bytes 524288 | tf_op jit(solution)/shard_map/all_to_all | solution.py:376
  217.6 5.2 %collective-permute-start.8 = (bf16[8,192,128]{2,1,0:T(8,128)(2,1)S(1)}, bf16[8,192,128]{2,1,0:T(8,128)(2,1)S(1)}, u32[]{:S(2)}, u32[]{:S(2)}) collective-permute-start(bf16[8,192,128]{2,1,0:T(8,128)(2,1)S(1)} %pad_maximum_fusion.6), channel_id=1, source_target_pairs={{0,8},{8,16},{16,24},{1,9},{9,17},{17,25},{2,10},{10,18},{18,26},{... | collective-permute-start | bytes 1179656 | tf_op jit(solution)/shard_map/ppermute | solution.py:27
  230.0 4.8 %collective-permute-start.10 = (bf16[8,8,32,128]{3,2,0,1:T(8,128)(2,1)S(1)}, bf16[8,8,32,128]{3,2,0,1:T(8,128)(2,1)}, u32[]{:S(2)}, u32[]{:S(2)}) collective-permute-start(bf16[8,8,32,128]{3,2,0,1:T(8,128)(2,1)S(1)} %pad_maximum_fusion.3), channel_id=1, source_target_pairs={{0,1},{1,2},{2,3},{3,4},{4,5},{5,6},{6,7},{8,9},{9,10},{10,11},{11... | collective-permute-start | bytes 1572872 | tf_op jit(solution)/shard_map/ppermute | solution.py:27
  237.2 9.4 %copy.56 = bf16[4,4,4,8,2,2,2048]{6,5,4,3,2,1,0:T(2,128)(2,1)} copy(bf16[4,4,4,8,2,2,2048]{6,3,5,4,2,0,1:T(8,128)(2,1)S(1)} %fusion) | data formatting | bytes 16777216 | tf_op jit(solution)/shard_map/convert_element_type | solution.py:447
  250.5 4.6 %fold_faces.1 = bf16[8,8,128,128]{3,2,1,0:T(8,128)(2,1)} custom-call(bf16[10,10,192,128]{3,2,1,0:T(8,128)(2,1)} %conv_input_grad.1.spread_0.spread_1, bf16[10,10,192,128]{3,2,1,0:T(8,128)(2,1)} %conv_input_grad.1.spread_0.spread_1, bf16[10,192,128]{2,1,0:T(8,128)(2,1)S(1)} %collective-permute-done.6.x_lo, ...), custom_call_target="tpu_custom_call" | custom-call | flops 100000000 | bytes 10485760 | tf_op jit(solution)/shard_map/fold_faces/pallas_call | solution.py:345
  (108 shorter events, 62.6 us)
Async XLA Ops:
  0.6 114.8 %copy-start = (f32[2048,256]{1,0:T(8,128)S(1)}, f32[2048,256]{1,0:T(8,128)}, u32[]{:S(2)}) copy-start(f32[2048,256]{1,0:T(8,128)} %param.9) | copy-start | bytes 6291460
  1.9 9.0 %collective-permute-start = (bf16[1,8,128,128]{3,2,1,0:T(8,128)(2,1)S(1)}, bf16[1,8,128,128]{3,2,1,0:T(8,128)(2,1)S(1)}, u32[]{:S(2)}, u32[]{:S(2)}) collective-permute-start(bf16[1,8,128,128]{3,2,1,0:T(8,128)(2,1)S(1)} %bitcast.235), channel_id=1, source_target_pairs={{0,32},{32,64},{64,96},{1,33},{33,65},{65,97},{2,34},{34,66},{66,9... | collective-permute-start | bytes 786440 | tf_op jit(solution)/shard_map/ppermute | solution.py:27
  5.9 8.8 %collective-permute-start.1 = (bf16[1,8,128,128]{3,2,1,0:T(8,128)(2,1)S(1)}, bf16[1,8,128,128]{3,2,1,0:T(8,128)(2,1)S(1)}, u32[]{:S(2)}, u32[]{:S(2)}) collective-permute-start(bf16[1,8,128,128]{3,2,1,0:T(8,128)(2,1)S(1)} %bitcast.234), channel_id=1, source_target_pairs={{32,0},{64,32},{96,64},{33,1},{65,33},{97,65},{34,2},{66,34},{98,6... | collective-permute-start | bytes 786440 | tf_op jit(solution)/shard_map/ppermute | solution.py:27
  7.2 26.4 %copy-start.4 = (bf16[3,3,3,32,64]{4,3,2,1,0:T(8,128)(2,1)S(1)}, bf16[3,3,3,32,64]{4,3,2,1,0:T(8,128)(2,1)}, u32[]{:S(2)}) copy-start(bf16[3,3,3,32,64]{4,3,2,1,0:T(8,128)(2,1)} %param.7) | copy-start | bytes 331780
  14.8 12.0 %collective-permute-start.3 = (bf16[10,1,128,128]{3,2,1,0:T(8,128)(2,1)S(1)}, bf16[10,1,128,128]{3,2,1,0:T(8,128)(2,1)S(1)}, u32[]{:S(2)}, u32[]{:S(2)}) collective-permute-start(bf16[10,1,128,128]{3,2,1,0:T(8,128)(2,1)S(1)} %pad_maximum_fusion.9), channel_id=1, source_target_pairs={{8,0},{16,8},{24,16},{9,1},{17,9},{25,17},{10,2},{18,10},{26,18},{... | collective-permute-start | bytes 983048 | tf_op jit(solution)/shard_map/ppermute | solution.py:27
  18.6 9.4 %collective-permute-start.2 = (bf16[10,1,128,128]{3,2,1,0:T(8,128)(2,1)S(1)}, bf16[10,1,128,128]{3,2,1,0:T(8,128)(2,1)S(1)}, u32[]{:S(2)}, u32[]{:S(2)}) collective-permute-start(bf16[10,1,128,128]{3,2,1,0:T(8,128)(2,1)S(1)} %pad_maximum_fusion.8), channel_id=1, source_target_pairs={{0,8},{8,16},{16,24},{1,9},{9,17},{17,25},{2,10},{10,18},{18,26},{... | collective-permute-start | bytes 983048 | tf_op jit(solution)/shard_map/ppermute | solution.py:27
  28.1 16.6 %collective-permute-start.5 = (bf16[10,10,32,128]{3,2,1,0:T(8,128)(2,1)S(1)}, bf16[10,10,32,128]{3,2,1,0:T(8,128)(2,1)S(1)}, u32[]{:S(2)}, u32[]{:S(2)}) collective-permute-start(bf16[10,10,32,128]{3,2,1,0:T(8,128)(2,1)S(1)} %pad_maximum_fusion.1), channel_id=1, source_target_pairs={{1,0},{2,1},{3,2},{4,3},{5,4},{6,5},{7,6},{9,8},{10,9},{11,10},{12... | collective-permute-start | bytes 2457608 | tf_op jit(solution)/shard_map/ppermute | solution.py:27
  29.6 17.0 %collective-permute-start.4 = (bf16[10,10,32,128]{3,2,1,0:T(8,128)(2,1)S(1)}, bf16[10,10,32,128]{3,2,1,0:T(8,128)(2,1)S(1)}, u32[]{:S(2)}, u32[]{:S(2)}) collective-permute-start(bf16[10,10,32,128]{3,2,1,0:T(8,128)(2,1)S(1)} %pad_maximum_fusion), channel_id=1, source_target_pairs={{0,1},{1,2},{2,3},{3,4},{4,5},{5,6},{6,7},{8,9},{9,10},{10,11},{11... | collective-permute-start | bytes 2457608 | tf_op jit(solution)/shard_map/ppermute | solution.py:27
  62.1 23.2 %all-to-all-start = ((bf16[32,64,128]{2,1,0:T(8,128)(2,1)}), bf16[32,64,128]{2,1,0:T(8,128)(2,1)S(1)}, u32[]{:S(2)}, u32[]{:S(2)}) async-start(bf16[32,64,128]{2,1,0:T(8,128)(2,1)} %copy.46), calls=%async_computation | async-start | bytes 1048576 | tf_op jit(solution)/shard_map/all_to_all | solution.py:376
  86.5 14.8 %copy-start.8 = (f32[4,128]{1,0:T(4,128)S(1)}, f32[4,128]{1,0:T(4,128)}, u32[]{:S(2)}) copy-start(f32[4,128]{1,0:T(4,128)} %param.11) | copy-start | bytes 6148
  91.2 25.1 %copy-start.9 = (f32[256,4]{0,1:T(4,128)S(1)}, f32[256,4]{0,1:T(4,128)}, u32[]{:S(2)}) copy-start(f32[256,4]{0,1:T(4,128)} %param.10) | copy-start | bytes 12292
  92.1 23.1 %all-to-all-start.1 = ((bf16[128,16,128]{2,1,0:T(8,128)(2,1)}), bf16[128,16,128]{2,1,0:T(8,128)(2,1)S(1)}, u32[]{:S(2)}, u32[]{:S(2)}) async-start(bf16[128,16,128]{2,1,0:T(8,128)(2,1)} %bitcast.87), calls=%async_computation.1 | async-start | bytes 1048576 | tf_op jit(solution)/shard_map/all_to_all | solution.py:376
  144.2 16.0 %all-to-all-start.3 = ((bf16[32,64,128]{2,1,0:T(8,128)(2,1)}), bf16[32,64,128]{2,1,0:T(8,128)(2,1)S(1)}, u32[]{:S(2)}, u32[]{:S(2)}) async-start(bf16[32,64,128]{2,1,0:T(8,128)(2,1)} %copy.51), calls=%async_computation.3 | async-start | bytes 1048576 | tf_op jit(solution)/shard_map/all_to_all | solution.py:376
  190.5 15.2 %all-to-all-start.4 = ((f32[128,4,128]{2,1,0:T(4,128)}), f32[128,4,128]{2,1,0:T(4,128)S(1)}, u32[]{:S(2)}, u32[]{:S(2)}) async-start(f32[128,4,128]{2,1,0:T(4,128)} %reshape.244), calls=%async_computation.4 | async-start | bytes 524288 | tf_op jit(solution)/shard_map/all_to_all | solution.py:376
  195.5 17.9 %collective-permute-start.6 = (bf16[10,192,128]{2,1,0:T(8,128)(2,1)}, bf16[10,192,128]{2,1,0:T(8,128)(2,1)S(1)}, u32[]{:S(2)}, u32[]{:S(2)}) collective-permute-start(bf16[10,192,128]{2,1,0:T(8,128)(2,1)} %get-tuple-element.29), channel_id=1, source_target_pairs={{0,32},{32,64},{64,96},{1,33},{33,65},{65,97},{2,34},{34,66},{66,9... | collective-permute-start | bytes 1474568 | tf_op jit(solution)/shard_map/ppermute | solution.py:27
  198.9 14.5 %collective-permute-start.7 = (bf16[10,192,128]{2,1,0:T(8,128)(2,1)}, bf16[10,192,128]{2,1,0:T(8,128)(2,1)S(1)}, u32[]{:S(2)}, u32[]{:S(2)}) collective-permute-start(bf16[10,192,128]{2,1,0:T(8,128)(2,1)} %get-tuple-element.28), channel_id=1, source_target_pairs={{32,0},{64,32},{96,64},{33,1},{65,33},{97,65},{34,2},{66,34},{98,6... | collective-permute-start | bytes 1474568 | tf_op jit(solution)/shard_map/ppermute | solution.py:27
  206.7 39.8 %all-to-all-start.5 = ((f32[128,4,128]{2,1,0:T(4,128)}), f32[128,4,128]{2,1,0:T(4,128)S(1)}, u32[]{:S(2)}, u32[]{:S(2)}) async-start(f32[128,4,128]{2,1,0:T(4,128)} %broadcast_in_dim.14), calls=%async_computation.5 | async-start | bytes 524288 | tf_op jit(solution)/shard_map/all_to_all | solution.py:376
  214.4 12.8 %collective-permute-start.9 = (bf16[8,192,128]{2,1,0:T(8,128)(2,1)S(1)}, bf16[8,192,128]{2,1,0:T(8,128)(2,1)S(1)}, u32[]{:S(2)}, u32[]{:S(2)}) collective-permute-start(bf16[8,192,128]{2,1,0:T(8,128)(2,1)S(1)} %pad_maximum_fusion.7), channel_id=1, source_target_pairs={{8,0},{16,8},{24,16},{9,1},{17,9},{25,17},{10,2},{18,10},{26,18},{... | collective-permute-start | bytes 1179656 | tf_op jit(solution)/shard_map/ppermute | solution.py:27
  217.5 17.3 %copy-start.3 = (bf16[32,64,128]{2,0,1:T(8,128)(2,1)S(1)}, bf16[32,64,128]{2,0,1:T(8,128)(2,1)}, u32[]{:S(2)}) copy-start(bf16[32,64,128]{2,0,1:T(8,128)(2,1)} %copy-done.2) | copy-start | bytes 1572868
  217.6 17.3 %copy-start.7 = (bf16[128,2048,1,1,1,1,1]{1,0,2,3,4,5,6:T(8,128)(2,1)S(1)}, bf16[128,2048,1,1,1,1,1]{1,0,2,3,4,5,6:T(8,128)(2,1)}, u32[]{:S(2)}) copy-start(bf16[128,2048,1,1,1,1,1]{1,0,2,3,4,5,6:T(8,128)(2,1)} %reshape.270) | copy-start | bytes 1572868
  217.6 9.9 %collective-permute-start.8 = (bf16[8,192,128]{2,1,0:T(8,128)(2,1)S(1)}, bf16[8,192,128]{2,1,0:T(8,128)(2,1)S(1)}, u32[]{:S(2)}, u32[]{:S(2)}) collective-permute-start(bf16[8,192,128]{2,1,0:T(8,128)(2,1)S(1)} %pad_maximum_fusion.6), channel_id=1, source_target_pairs={{0,8},{8,16},{16,24},{1,9},{9,17},{17,25},{2,10},{10,18},{18,26},{... | collective-permute-start | bytes 1179656 | tf_op jit(solution)/shard_map/ppermute | solution.py:27
  227.2 7.6 %copy-start.5 = (bf16[8,192,128]{2,1,0:T(8,128)(2,1)}, bf16[8,192,128]{2,1,0:T(8,128)(2,1)S(1)}, u32[]{:S(2)}) copy-start(bf16[8,192,128]{2,1,0:T(8,128)(2,1)S(1)} %collective-permute-done.9.y_hi) | copy-start | bytes 1179652
  228.4 22.0 %collective-permute-start.11 = (bf16[8,8,32,128]{3,2,1,0:T(8,128)(2,1)}, bf16[8,8,32,128]{3,2,1,0:T(8,128)(2,1)}, u32[]{:S(2)}, u32[]{:S(2)}) collective-permute-start(bf16[8,8,32,128]{3,2,1,0:T(8,128)(2,1)} %pad_maximum_fusion.5), channel_id=1, source_target_pairs={{1,0},{2,1},{3,2},{4,3},{5,4},{6,5},{7,6},{9,8},{10,9},{11,10},{12... | collective-permute-start | bytes 1572872 | tf_op jit(solution)/shard_map/ppermute | solution.py:27
  230.0 18.4 %collective-permute-start.10 = (bf16[8,8,32,128]{3,2,0,1:T(8,128)(2,1)S(1)}, bf16[8,8,32,128]{3,2,0,1:T(8,128)(2,1)}, u32[]{:S(2)}, u32[]{:S(2)}) collective-permute-start(bf16[8,8,32,128]{3,2,0,1:T(8,128)(2,1)S(1)} %pad_maximum_fusion.3), channel_id=1, source_target_pairs={{0,1},{1,2},{2,3},{3,4},{4,5},{5,6},{6,7},{8,9},{9,10},{10,11},{11... | collective-permute-start | bytes 1572872 | tf_op jit(solution)/shard_map/ppermute | solution.py:27
  (3 other events, 14.8 us)
where the time goes:
time: 258 us; the launch traced here: 255 us
  starting transfers between devices  73.2 us (28%)
  local copies, waits for them, and re-layouts  49 us (19%)
  waiting for transfers between devices  46.9 us (18%)
  Pallas kernels  45.2 us (18%)
  blocking collectives  17.9 us (7%)
  matrix products  16.3 us (6%)
  other arithmetic  5.4 us (2%)
    all_to_all x5, starting transfers between devices, exchange(): return lax.all_to_all(array, axes, split_axis=0, concat_axis=0, tiled=True)  34.2 us
    ppermute x6, starting transfers between devices, both_ways(): lax.ppermute(toward_up, axis, up)  26.8 us
    all_to_all x5, waiting for transfers between devices, exchange(): return lax.all_to_all(array, axes, split_axis=0, concat_axis=0, tiled=True)  22.4 us
    ppermute x6, waiting for transfers between devices, both_ways(): lax.ppermute(toward_down, axis, down)  19.9 us
    all_to_all x1, blocking collectives, exchange(): return lax.all_to_all(array, axes, split_axis=0, concat_axis=0, tiled=True)  17.9 us
    pallas_call x1, Pallas kernels, forward_call(): pl.pallas_call(body, grid=(nx // 2,), in_specs=[whole(a) for a in operand...  14.4 us
    pallas_call x1, Pallas kernels, input_grad_call(): pl.pallas_call(body, grid=(nx // 2 + 1,), in_specs=[pl.BlockSpec((2, ny,...  14.1 us
    reshape x1, local copies, waits for them, and re-layouts, body(): dense_one.reshape(-1, dense_one.shape[4])  13.1 us
  transfers between devices with their start and end apart: 17, of which 11 were waited for; matrix products, arithmetic and copies ran while one was open for 18% of the time, Pallas kernels for 0%

commit v1 on v0

--- a/solution.py
+++ b/solution.py
@@ -35,31 +35,18 @@
     return leak_slope + (1.0 - leak_slope) * jax.nn.sigmoid(values)
 
 
-def banded_kernel(kernel, cells):
-    taps_x, taps_y, _, c_in, c_out = kernel.shape
-    bands = [
-        jnp.pad(kernel, ((0, 0), (0, 0), (z, cells - 1 - z), (0, 0), (0, 0)))
-        for z in range(cells)
-    ]
-    whole = jnp.stack(bands)
-    return jnp.transpose(whole, (3, 4, 1, 2, 0, 5)).reshape(
-        (cells + 2) * c_in, taps_x * taps_y * cells * c_out
-    )
-
-
-def forward_call(core, x_lo, x_hi, y_lo, y_hi, z_lo, z_hi, twice):
-    nx, ny, width, lanes = core.shape
-    edge = z_lo.shape[2]
-    depth = width + 2 * edge
-    half = twice.shape[1] // 2
-    rows = 4 * half
-    tap = 3 * edge
-
-    def build(twice, matrix):
-        for pair in range(2):
+def banded_matrices(twice, cells, c_in):
+    lanes = twice.shape[1]
+    half = lanes // 2
+    tap = 3 * c_in
+    depth = (cells + 2) * c_in
+    rows = cells * half
+
+    def body(twice, forward, backward):
+        side = lax.broadcasted_iota(jnp.int32, (tap, lanes), 1) < half
+        for pair in range(cells // 2):
             for start in range(0, 9, 2):
                 count = min(2, 9 - start)
-                side = lax.broadcasted_iota(jnp.int32, (tap, 2 * half), 1) < half
                 blocks = []
                 for k in range(start, start + count):
                     block = twice[k * tap : (k + 1) * tap, :]
@@ -71,18 +58,40 @@
                 from_row = lax.broadcasted_iota(jnp.int32, (size, size), 1)
                 which = from_row // tap
                 moved = (
-                    (which // 2) * depth + (2 * pair + which % 2) * edge + from_row - which * tap
+                    (which // 2) * depth + (2 * pair + which % 2) * c_in + from_row - which * tap
                 )
                 place = jnp.where(here == moved, 1.0, 0.0).astype(bf16)
-                matrix[
-                    pair * 2 * half : (pair + 1) * 2 * half,
-                    start * depth : (start + count) * depth,
+                forward[
+                    pair * lanes : (pair + 1) * lanes, start * depth : (start + count) * depth
                 ] = lax.dot_general(
                     stacked, place, (((0,), (1,)), ((), ())), preferred_element_type=f32
                 ).astype(bf16)
+                both = jnp.dot(place, stacked, preferred_element_type=f32).astype(bf16)
+                for k in range(count):
+                    at = (start + k) * rows + pair * lanes
+                    backward[:, at : at + lanes] = both[k * depth : (k + 1) * depth]
+
+    return pl.pallas_call(
+        body,
+        out_shape=[
+            jax.ShapeDtypeStruct((rows, 9 * depth), bf16),
+            jax.ShapeDtypeStruct((depth, 9 * rows), bf16),
+        ],
+        compiler_params=pltpu.CompilerParams(vmem_limit_bytes=16 * 2**20),
+        cost_estimate=pl.CostEstimate(flops=10**9, bytes_accessed=2**21, transcendentals=0),
+        name="banded_matrices",
+    )(twice)
+
+
+def forward_call(core, x_lo, x_hi, y_lo, y_hi, z_lo, z_hi, matrix):
+    nx, ny, width, lanes = core.shape
+    edge = z_lo.shape[2]
+    depth = width + 2 * edge
+    rows = matrix.shape[0]
+    half = rows // 4
 
     def body(
-        core, x_lo, x_hi, y_lo, y_hi, z_lo, z_hi, twice, kept, conv_out, pooled, padded, matrix, sem
+        core, x_lo, x_hi, y_lo, y_hi, z_lo, z_hi, matrix, kept, conv_out, pooled, padded, sem
     ):
         step = pl.program_id(0)
 
@@ -97,12 +106,11 @@
             padded[:, :, 0:edge, :] = z_lo[...]
             padded[:, :, edge + width : depth, :] = z_hi[...]
             pltpu.make_async_copy(padded, kept, sem).start()
-            build(twice, matrix)
 
         weights = matrix[...]
         for pair in range(ny // 2):
             y = 2 * pair
-            total = None
+            total, factor = 0.0, 1.0
             for inner in range(2):
                 x = 2 * step + inner
                 patch = jnp.concatenate(
@@ -118,13 +126,15 @@
                 values = jnp.dot(weights, patch, preferred_element_type=f32)
                 conv_out[inner, y] = values[:, :lanes].astype(bf16)
                 conv_out[inner, y + 1] = values[:, lanes:].astype(bf16)
-                soft = jnp.maximum(values, 0.0) + jnp.log(1.0 + jnp.exp(-jnp.abs(values)))
-                acted = leak_slope * values + (1.0 - leak_slope) * soft
-                across = acted[:, :lanes] + acted[:, lanes:]
-                total = across if total is None else total + across
-            total = total * 0.125
-            pooled[0, pair, 0] = (total[:half] + total[half : 2 * half]).astype(bf16)
-            pooled[0, pair, 1] = (total[2 * half : 3 * half] + total[3 * half :]).astype(bf16)
+                straight = jnp.maximum(leak_slope * values, values)
+                grown = 1.0 + jnp.exp(-jnp.abs(values))
+                total = total + (straight[:, :lanes] + straight[:, lanes:])
+                factor = factor * (grown[:, :lanes] * grown[:, lanes:])
+            for z in range(2):
+                low, high = 2 * z * half, (2 * z + 1) * half
+                bent = jnp.log(factor[low : low + half] * factor[high : high + half])
+                mean = 0.125 * (total[low : low + half] + total[high : high + half])
+                pooled[0, pair, z] = (mean + (0.125 * (1.0 - leak_slope)) * bent).astype(bf16)
 
         @pl.when(step == nx // 2 - 1)
         def _():
@@ -133,7 +143,7 @@
     def whole(array):
         return pl.BlockSpec(array.shape, lambda i: (0,) * array.ndim)
 
-    operands = (in_hbm(core), x_lo, x_hi, y_lo, y_hi, z_lo, z_hi, twice)
+    operands = (in_hbm(core), x_lo, x_hi, y_lo, y_hi, z_lo, z_hi, matrix)
     padded_shape = (nx + 2, ny + 2, depth, lanes)
     return pl.pallas_call(
         body,
@@ -151,7 +161,6 @@
         ],
         scratch_shapes=[
             pltpu.VMEM(padded_shape, bf16),
-            pltpu.VMEM((rows, 9 * depth), bf16),
             pltpu.SemaphoreType.DMA,
         ],
         compiler_params=pltpu.CompilerParams(vmem_limit_bytes=40 * 2**20),
@@ -237,7 +246,7 @@
     nx, ny, rows, lanes = grad_out.shape
     depth = matrix.shape[0]
 
-    def body(grad_out, matrix, spread, held):
+    def body(grad_out, matrix, spread, faces, held):
         step = pl.program_id(0)
 
         @pl.when(step == 0)
@@ -277,6 +286,7 @@
                 values = values.astype(bf16)
                 spread[x, y] = values[:, :lanes]
                 spread[x, y + 1] = values[:, lanes:]
+        faces[0] = jnp.where(step == 0, spread[0], spread[1])
 
     return pl.pallas_call(
         body,
@@ -285,8 +295,14 @@
             pl.BlockSpec((2, ny, rows, lanes), lambda i: (jnp.minimum(i, nx // 2 - 1), 0, 0, 0)),
             pl.BlockSpec(matrix.shape, lambda i: (0, 0)),
         ],
-        out_specs=pl.BlockSpec((2, ny + 2, depth, lanes), lambda i: (i, 0, 0, 0)),
-        out_shape=pltpu.HBM((nx + 2, ny + 2, depth, lanes), bf16),
+        out_specs=[
+            pl.BlockSpec((2, ny + 2, depth, lanes), lambda i: (i, 0, 0, 0)),
+            pl.BlockSpec((1, ny + 2, depth, lanes), lambda i: (jnp.minimum(i, 1), 0, 0, 0)),
+        ],
+        out_shape=[
+            pltpu.HBM((nx + 2, ny + 2, depth, lanes), bf16),
+            jax.ShapeDtypeStruct((2, ny + 2, depth, lanes), bf16),
+        ],
         scratch_shapes=[pltpu.VMEM((nx + 4, ny + 4, rows, lanes), bf16)],
         compiler_params=pltpu.CompilerParams(vmem_limit_bytes=40 * 2**20),
         cost_estimate=pl.CostEstimate(flops=9 * 10**9, bytes_accessed=12 * 2**20, transcendentals=0),
@@ -372,6 +388,31 @@
     )
 
 
+def feature_grad_call(weights, grad_pre_one):
+    features, units = weights.shape
+    samples = grad_pre_one.shape[0]
+    block = features // 4
+
+    def body(weights, grad, result):
+        result[...] = lax.dot_general(
+            weights[...], grad[...], (((1,), (1,)), ((), ())), preferred_element_type=f32
+        ).astype(bf16)
+
+    return pl.pallas_call(
+        body,
+        grid=(features // block,),
+        in_specs=[
+            pl.BlockSpec((block, units), lambda i: (i, 0)),
+            pl.BlockSpec((samples, units), lambda i: (0, 0)),
+        ],
+        out_specs=pl.BlockSpec((block, samples), lambda i: (i, 0)),
+        out_shape=jax.ShapeDtypeStruct((features, samples), bf16),
+        compiler_params=pltpu.CompilerParams(vmem_limit_bytes=16 * 2**20),
+        cost_estimate=pl.CostEstimate(flops=10**9, bytes_accessed=10 * 2**20, transcendentals=0),
+        name="feature_grad",
+    )(in_hbm(weights), grad_pre_one)
+
+
 def exchange(array, axes):
     return lax.all_to_all(array, axes, split_axis=0, concat_axis=0, tiled=True)
 
@@ -397,11 +438,11 @@
         return jnp.concatenate([sides[0], middle, sides[4]], axis=1)
 
     z_lo, z_hi = both_ways(z_layer(slice(-c_in, None)), z_layer(slice(0, c_in)), "gz")
-    backward_matrix = banded_kernel(conv_kernel, nz)
     twice = conv_kernel.reshape(-1, c_out)
     twice = jnp.concatenate([twice, twice], axis=1)
+    forward_matrix, backward_matrix = banded_matrices(twice, nz, c_in)
     padded, conv_out, pooled = forward_call(
-        core, x_lo[0], x_hi[0], y_lo[:, 0], y_hi[:, 0], z_lo, z_hi, twice
+        core, x_lo[0], x_hi[0], y_lo[:, 0], y_hi[:, 0], z_lo, z_hi, forward_matrix
     )
 
     half_x, half_y, half_z = nx // 2, ny // 2, nz // 2
@@ -409,8 +450,10 @@
     outgoing = pooled.reshape(cells, groups, per_group, samples).transpose(1, 0, 2, 3)
     arrived = exchange(outgoing.reshape(groups, cells * per_group, samples), ("gy", "gz"))
     arrived = arrived.reshape(groups_y, groups_z, half_x, half_y, half_z, per_group, samples)
-    features = arrived.transpose(2, 0, 3, 1, 4, 5, 6).reshape(-1, samples)
-    weights = lax.optimization_barrier(dense_one.reshape(-1, dense_one.shape[4]))
+    features = arrived.transpose(2, 0, 3, 5, 1, 4, 6).reshape(-1, samples)
+    weights = lax.optimization_barrier(
+        dense_one.transpose(0, 1, 3, 2, 4).reshape(-1, dense_one.shape[4])
+    )
     partial_one = lax.dot_general(
         features, weights, (((0,), (0,)), ((), ())), preferred_element_type=f32
     )
@@ -434,12 +477,10 @@
     copies = jnp.broadcast_to(own_grad.reshape(1, rows, 128), (devices, rows, 128))
     grad_pre_one = exchange(copies, everyone).reshape(samples, rows * 128)
 
-    grad_features = lax.dot_general(
-        weights, grad_pre_one, (((1,), (1,)), ((), ())), preferred_element_type=f32
-    ).astype(bf16)
+    grad_features = feature_grad_call(weights, grad_pre_one)
     grad_features = grad_features.reshape(
-        half_x, groups_y, half_y, groups_z, half_z, per_group, samples
-    ).transpose(1, 3, 0, 2, 4, 5, 6)
+        half_x, groups_y, half_y, per_group, groups_z, half_z, samples
+    ).transpose(1, 4, 0, 2, 5, 3, 6)
     returned = exchange(grad_features.reshape(groups, cells * per_group, samples), ("gy", "gz"))
     grad_dense_one = (
         jnp.einsum("uvxyzcb,bh->xuyvzch", arrived, grad_pre_one, preferred_element_type=f32)
@@ -450,8 +491,8 @@
     ).reshape(pooled.shape)
 
     grad_out, kernel_local = kernel_grad_call(padded, conv_out, grad_pooled, c_in)
-    spread = input_grad_call(grad_out, backward_matrix)
-    from_lo, from_hi = both_ways(spread[-1], spread[0], "gx")
+    spread, x_faces = input_grad_call(grad_out, backward_matrix)
+    from_lo, from_hi = both_ways(x_faces[1], x_faces[0], "gx")
 
     def added(array, first_term, last_term):
         head = (array[:1].astype(f32) + first_term.astype(f32)).astype(bf16)

time: 258 us -> 256 us (level)
  waiting for transfers between devices: 46.9 us -> 56.6 us
  local copies, waits for them, and re-layouts: 49 us -> 40.1 us
  matrix products: 16.3 us -> 10 us
  Pallas kernels: 45.2 us -> 50.7 us
    reshape x2 -> x1, local copies, waits for them, and re-layouts: 16.1 us -> 0.11 us  [body(): grad_features.reshape(half_x, groups_y, half_y, per_group, groups_z, half...]
    all_to_all x5, waiting for transfers between devices: 22.4 us -> 33.4 us  [exchange(): return lax.all_to_all(array, axes, split_axis=0, concat_axis=0, tiled=True)]
    transpose x3 -> x2, local copies, waits for them, and re-layouts: 3.18 us -> 12.2 us  [the longest x1 11.4 us: body(): dense_one.transpose(0, 1, 3, 2, 4).reshape(-1, dense_one.shape[4])]
    pallas_call x0 -> x2, Pallas kernels: none -> 6.99 us  [the longest x1 5.51 us: feature_grad_call(): pl.pallas_call(body, grid=(features // block,), in_specs=[pl.BlockSpec((b...]
    dot_general x1 -> x0, matrix products: 6.27 us -> none  [body(): lax.dot_general(weights, grad_pre_one, (((1,), (1,)), ((), ())), preferre...]
  transfers between devices with their start and end apart: 17 -> 17, of which waited for: 11 -> 11; matrix products, arithmetic and copies ran while one was open for 18% -> 16% of each run, Pallas kernels for 0% -> 1%
where the time goes in v1:
time: 256 us; the launch traced here: 254 us
  starting transfers between devices  72.1 us (28%)
  waiting for transfers between devices  56.6 us (22%)
  Pallas kernels  50.7 us (20%)
  local copies, waits for them, and re-layouts  40.1 us (16%)
  blocking collectives  17.9 us (7%)
  matrix products  10 us (4%)
  other arithmetic  5.12 us (2%)
    all_to_all x5, starting transfers between devices, exchange(): return lax.all_to_all(array, axes, split_axis=0, concat_axis=0, tiled=True)  35.3 us
    all_to_all x5, waiting for transfers between devices, exchange(): return lax.all_to_all(array, axes, split_axis=0, concat_axis=0, tiled=True)  33.4 us
    ppermute x6, starting transfers between devices, both_ways(): lax.ppermute(toward_up, axis, up)  24.9 us
    ppermute x6, waiting for transfers between devices, both_ways(): lax.ppermute(toward_down, axis, down)  18.8 us
    all_to_all x1, blocking collectives, exchange(): return lax.all_to_all(array, axes, split_axis=0, concat_axis=0, tiled=True)  17.9 us
    pallas_call x1, Pallas kernels, input_grad_call(): pl.pallas_call(body, grid=(nx // 2 + 1,), in_specs=[pl.BlockSpec((2, ny,...  14.5 us
    pallas_call x1, Pallas kernels, forward_call(): pl.pallas_call(body, grid=(nx // 2,), in_specs=[whole(a) for a in operand...  12.5 us
    pallas_call x1, Pallas kernels, kernel_grad_call(): pl.pallas_call(body, grid=(nx // 2,), in_specs=[pl.BlockSpec((2,) + padde...  12.1 us
  transfers between devices with their start and end apart: 17, of which 11 were waited for; matrix products, arithmetic and copies ran while one was open for 16% of the time, Pallas kernels for 1%

profile of v1, /device:TPU:1, one launch (start us, length us, event | category | flops | bytes accessed | tf_op | source)
XLA Modules:
  0.0 253.7 jit_solution(29888802469690598)
XLA Ops:
  1.9 4.0 %collective-permute-start = (bf16[1,8,128,128]{3,2,1,0:T(8,128)(2,1)S(1)}, bf16[1,8,128,128]{3,2,1,0:T(8,128)(2,1)S(1)}, u32[]{:S(2)}, u32[]{:S(2)}) collective-permute-start(bf16[1,8,128,128]{3,2,1,0:T(8,128)(2,1)S(1)} %bitcast.208), channel_id=1, source_target_pairs={{0,32},{32,64},{64,96},{1,33},{33,65},{65,97},{2,34},{34,66},{66,9... | collective-permute-start | bytes 786440 | tf_op jit(solution)/shard_map/ppermute | solution.py:27
  10.9 3.8 %collective-permute-done.1 = bf16[1,8,128,128]{3,2,1,0:T(8,128)(2,1)S(1)} collective-permute-done((bf16[1,8,128,128]{3,2,1,0:T(8,128)(2,1)S(1)}, bf16[1,8,128,128]{3,2,1,0:T(8,128)(2,1)S(1)}, u32[]{:S(2)}, u32[]{:S(2)}) %collective-permute-start.1) | collective-permute-done | bytes 262176 | tf_op jit(solution)/shard_map/ppermute | solution.py:27
  18.6 5.4 %collective-permute-start.2 = (bf16[10,1,128,128]{3,2,1,0:T(8,128)(2,1)S(1)}, bf16[10,1,128,128]{3,2,1,0:T(8,128)(2,1)S(1)}, u32[]{:S(2)}, u32[]{:S(2)}) collective-permute-start(bf16[10,1,128,128]{3,2,1,0:T(8,128)(2,1)S(1)} %pad_maximum_fusion.8), channel_id=1, source_target_pairs={{0,8},{8,16},{16,24},{1,9},{9,17},{17,25},{2,10},{10,18},{18,26},{... | collective-permute-start | bytes 983048 | tf_op jit(solution)/shard_map/ppermute | solution.py:27
  29.6 4.0 %collective-permute-start.4 = (bf16[10,10,32,128]{3,2,1,0:T(8,128)(2,1)S(1)}, bf16[10,10,32,128]{3,2,1,0:T(8,128)(2,1)S(1)}, u32[]{:S(2)}, u32[]{:S(2)}) collective-permute-start(bf16[10,10,32,128]{3,2,1,0:T(8,128)(2,1)S(1)} %pad_maximum_fusion), channel_id=1, source_target_pairs={{0,1},{1,2},{2,3},{3,4},{4,5},{5,6},{6,7},{8,9},{9,10},{10,11},{11... | collective-permute-start | bytes 2457608 | tf_op jit(solution)/shard_map/ppermute | solution.py:27
  35.3 9.4 %collective-permute-done.5.z_hi = bf16[10,10,32,128]{3,2,1,0:T(8,128)(2,1)S(1)} collective-permute-done((bf16[10,10,32,128]{3,2,1,0:T(8,128)(2,1)S(1)}, bf16[10,10,32,128]{3,2,1,0:T(8,128)(2,1)S(1)}, u32[]{:S(2)}, u32[]{:S(2)}) %collective-permute-start.5) | collective-permute-done | bytes 819232 | tf_op jit(solution)/shard_map/ppermute | solution.py:27
  46.6 12.5 %conv_forward.1 = (bf16[10,10,192,128]{3,2,1,0:T(8,128)(2,1)}, bf16[8,8,256,128]{3,2,1,0:T(8,128)(2,1)}, bf16[4,4,2,64,128]{4,3,2,1,0:T(8,128)(2,1)S(1)}) custom-call(bf16[8,8,128,128]{3,2,1,0:T(8,128)(2,1)} %bitcast.197, bf16[8,128,128]{2,1,0:T(8,128)(2,1)S(1)} %bitcast.184, bf16[8,128,128]{2,1,0:T(8,128)(2,1)S(1)} %bitcast.185, ...), custom_call_target="tpu_custom_call" | custom-call | flops 7000000000 | bytes 16777216 | tf_op jit(solution)/shard_map/conv_forward/pallas_call | solution.py:148
  60.3 10.2 %all-to-all-start = ((bf16[32,64,128]{2,1,0:T(8,128)(2,1)}), bf16[32,64,128]{2,1,0:T(8,128)(2,1)S(1)}, u32[]{:S(2)}, u32[]{:S(2)}) async-start(bf16[32,64,128]{2,1,0:T(8,128)(2,1)} %copy.46), calls=%async_computation | async-start | bytes 1048576 | tf_op jit(solution)/shard_map/all_to_all | solution.py:417
  70.5 11.4 %copy.44 = bf16[4,16,2,16,2048]{4,3,2,1,0:T(8,128)(2,1)} copy(bf16[4,16,2,16,2048]{4,2,3,1,0:T(2,128)(2,1)} %bitcast.190) | data formatting | bytes 16777216 | tf_op jit(solution)/shard_map/transpose | solution.py:455
  83.2 4.7 %fusion.1 = bf16[16,8,16,128]{3,1,2,0:T(8,128)(2,1)S(1)} fusion(bf16[2048,128]{1,0:T(8,128)(2,1)S(1)} %bitcast.193, bf16[2048,2048]{1,0:T(8,128)(2,1)} %bitcast.188), kind=kOutput, calls=%fused_computation.3 | convolution fusion | flops 1074003968 | bytes 9437184 | tf_op jit(solution)/shard_map/dot_general | solution.py:457
  88.8 9.0 %all-to-all-start.1 = ((bf16[128,16,128]{2,1,0:T(8,128)(2,1)}), bf16[128,16,128]{2,1,0:T(8,128)(2,1)S(1)}, u32[]{:S(2)}, u32[]{:S(2)}) async-start(bf16[128,16,128]{2,1,0:T(8,128)(2,1)} %bitcast.200), calls=%async_computation.1 | async-start | bytes 1048576 | tf_op jit(solution)/shard_map/all_to_all | solution.py:417
  98.0 13.8 %all-to-all-done.1 = bf16[128,16,128]{2,1,0:T(8,128)(2,1)S(1)} async-done(((bf16[128,16,128]{2,1,0:T(8,128)(2,1)}), bf16[128,16,128]{2,1,0:T(8,128)(2,1)S(1)}, u32[]{:S(2)}, u32[]{:S(2)}) %all-to-all-start.1) | async-done | bytes 524320 | tf_op jit(solution)/shard_map/all_to_all | solution.py:417
  115.1 17.9 %all_to_all.30 = bf16[128,16,128]{2,1,0:T(8,128)(2,1)S(1)} all-to-all(bf16[128,16,128]{2,1,0:T(8,128)(2,1)S(1)} %broadcast_in_dim.11), channel_id=1, replica_groups=mesh['gx'=4,'gy'=4,'gz'=8] {'gx','gy','gz'}, dimensions={0} | all-to-all | bytes 1048576 | tf_op jit(solution)/shard_map/all_to_all | solution.py:417
  133.1 5.5 %feature_grad.1 = bf16[2048,128]{1,0:T(8,128)(2,1)S(1)} custom-call(bf16[2048,2048]{1,0:T(8,128)(2,1)} %bitcast.189, bf16[128,2048]{1,0:T(8,128)(2,1)S(1)} %bitcast.181), custom_call_target="tpu_custom_call" | custom-call | flops 1000000000 | bytes 10485760 | tf_op jit(solution)/shard_map/feature_grad/pallas_call | solution.py:401
  139.7 4.4 %all-to-all-start.3 = ((bf16[32,64,128]{2,1,0:T(8,128)(2,1)}), bf16[32,64,128]{2,1,0:T(8,128)(2,1)S(1)}, u32[]{:S(2)}, u32[]{:S(2)}) async-start(bf16[32,64,128]{2,1,0:T(8,128)(2,1)} %copy.50), calls=%async_computation.3 | async-start | bytes 1048576 | tf_op jit(solution)/shard_map/all_to_all | solution.py:417
  145.2 10.6 %all-to-all-done.3 = bf16[32,64,128]{2,1,0:T(8,128)(2,1)S(1)} async-done(((bf16[32,64,128]{2,1,0:T(8,128)(2,1)}), bf16[32,64,128]{2,1,0:T(8,128)(2,1)S(1)}, u32[]{:S(2)}, u32[]{:S(2)}) %all-to-all-start.3) | async-done | bytes 524320 | tf_op jit(solution)/shard_map/all_to_all | solution.py:417
  156.6 12.1 %conv_kernel_grad.1 = (bf16[8,8,256,128]{3,2,1,0:T(8,128)(2,1)}, f32[27,32,64]{2,1,0:T(8,128)S(1)}) custom-call(bf16[10,10,192,128]{3,2,1,0:T(8,128)(2,1)} %get-tuple-element.14.rows_0.rows_1, bf16[10,10,192,128]{3,2,1,0:T(8,128)(2,1)} %get-tuple-element.14.rows_0.rows_1, bf16[8,8,256,128]{3,2,1,0:T(8,128)(2,1)} %get-tuple-element.15.conv_out, ...), custom_call_target="tpu_custom_call" | custom-call | flops 8000000000 | bytes 14680064 | tf_op jit(solution)/shard_map/conv_kernel_grad/pallas_call | solution.py:221
  168.8 14.5 %conv_input_grad.1 = (bf16[10,10,192,128]{3,2,1,0:T(8,128)(2,1)}, bf16[2,10,192,128]{3,2,1,0:T(8,128)(2,1)S(1)}) custom-call(bf16[8,8,256,128]{3,2,1,0:T(8,128)(2,1)} %get-tuple-element.18.grad_out, bf16[192,2304]{1,0:T(8,128)(2,1)S(1)} %get-tuple-element.19.matrix), custom_call_target="tpu_custom_call" | custom-call | flops 8999999488 | bytes 12582912 | tf_op jit(solution)/shard_map/conv_input_grad/pallas_call | solution.py:291
  188.9 6.0 %all-to-all-start.4 = ((f32[128,4,128]{2,1,0:T(4,128)}), f32[128,4,128]{2,1,0:T(4,128)S(1)}, u32[]{:S(2)}, u32[]{:S(2)}) async-start(f32[128,4,128]{2,1,0:T(4,128)} %reshape.241), calls=%async_computation.4 | async-start | bytes 524288 | tf_op jit(solution)/shard_map/all_to_all | solution.py:417
  197.2 8.9 %all-to-all-done.4 = f32[128,4,128]{2,1,0:T(4,128)S(1)} async-done(((f32[128,4,128]{2,1,0:T(4,128)}), f32[128,4,128]{2,1,0:T(4,128)S(1)}, u32[]{:S(2)}, u32[]{:S(2)}) %all-to-all-start.4) | async-done | bytes 262176 | tf_op jit(solution)/shard_map/all_to_all | solution.py:417
  207.1 5.7 %all-to-all-start.5 = ((f32[128,4,128]{2,1,0:T(4,128)}), f32[128,4,128]{2,1,0:T(4,128)S(1)}, u32[]{:S(2)}, u32[]{:S(2)}) async-start(f32[128,4,128]{2,1,0:T(4,128)} %broadcast_in_dim.14), calls=%async_computation.5 | async-start | bytes 524288 | tf_op jit(solution)/shard_map/all_to_all | solution.py:417
  217.0 4.4 %collective-permute-start.8 = (bf16[8,192,128]{2,1,0:T(8,128)(2,1)S(1)}, bf16[8,192,128]{2,1,0:T(8,128)(2,1)S(1)}, u32[]{:S(2)}, u32[]{:S(2)}) collective-permute-start(bf16[8,192,128]{2,1,0:T(8,128)(2,1)S(1)} %pad_maximum_fusion.6), channel_id=1, source_target_pairs={{0,8},{8,16},{16,24},{1,9},{9,17},{17,25},{2,10},{10,18},{18,26},{... | collective-permute-start | bytes 1179656 | tf_op jit(solution)/shard_map/ppermute | solution.py:27
  228.6 4.8 %collective-permute-start.10 = (bf16[8,8,32,128]{3,2,0,1:T(8,128)(2,1)S(1)}, bf16[8,8,32,128]{3,2,0,1:T(8,128)(2,1)}, u32[]{:S(2)}, u32[]{:S(2)}) collective-permute-start(bf16[8,8,32,128]{3,2,0,1:T(8,128)(2,1)S(1)} %pad_maximum_fusion.3), channel_id=1, source_target_pairs={{0,1},{1,2},{2,3},{3,4},{4,5},{5,6},{6,7},{8,9},{9,10},{10,11},{11... | collective-permute-start | bytes 1572872 | tf_op jit(solution)/shard_map/ppermute | solution.py:27
  235.7 9.4 %copy.55 = bf16[4,4,4,8,2,2,2048]{6,5,4,3,2,1,0:T(2,128)(2,1)} copy(bf16[4,4,4,8,2,2,2048]{6,3,5,4,2,0,1:T(8,128)(2,1)S(1)} %fusion) | data formatting | bytes 16777216 | tf_op jit(solution)/shard_map/convert_element_type | solution.py:488
  249.1 4.6 %fold_faces.1 = bf16[8,8,128,128]{3,2,1,0:T(8,128)(2,1)} custom-call(bf16[10,10,192,128]{3,2,1,0:T(8,128)(2,1)} %get-tuple-element.20.spread_0.spread_1, bf16[10,10,192,128]{3,2,1,0:T(8,128)(2,1)} %get-tuple-element.20.spread_0.spread_1, bf16[10,192,128]{2,1,0:T(8,128)(2,1)S(1)} %collective-permute-done.6.x_lo, ...), custom_call_target="tpu_custom_call" | custom-call | flops 100000000 | bytes 10485760 | tf_op jit(solution)/shard_map/fold_faces/pallas_call | solution.py:361
  (105 shorter events, 55.4 us)
Async XLA Ops:
  0.6 111.3 %copy-start = (f32[2048,256]{1,0:T(8,128)S(1)}, f32[2048,256]{1,0:T(8,128)}, u32[]{:S(2)}) copy-start(f32[2048,256]{1,0:T(8,128)} %param.9) | copy-start | bytes 6291460
  0.6 33.0 %copy-start.7 = (bf16[3,3,3,32,64]{4,3,2,1,0:T(8,128)(2,1)S(1)}, bf16[3,3,3,32,64]{4,3,2,1,0:T(8,128)(2,1)}, u32[]{:S(2)}) copy-start(bf16[3,3,3,32,64]{4,3,2,1,0:T(8,128)(2,1)} %param.7) | copy-start | bytes 331780
  1.9 9.0 %collective-permute-start = (bf16[1,8,128,128]{3,2,1,0:T(8,128)(2,1)S(1)}, bf16[1,8,128,128]{3,2,1,0:T(8,128)(2,1)S(1)}, u32[]{:S(2)}, u32[]{:S(2)}) collective-permute-start(bf16[1,8,128,128]{3,2,1,0:T(8,128)(2,1)S(1)} %bitcast.208), channel_id=1, source_target_pairs={{0,32},{32,64},{64,96},{1,33},{33,65},{65,97},{2,34},{34,66},{66,9... | collective-permute-start | bytes 786440 | tf_op jit(solution)/shard_map/ppermute | solution.py:27
  5.9 8.8 %collective-permute-start.1 = (bf16[1,8,128,128]{3,2,1,0:T(8,128)(2,1)S(1)}, bf16[1,8,128,128]{3,2,1,0:T(8,128)(2,1)S(1)}, u32[]{:S(2)}, u32[]{:S(2)}) collective-permute-start(bf16[1,8,128,128]{3,2,1,0:T(8,128)(2,1)S(1)} %bitcast.207), channel_id=1, source_target_pairs={{32,0},{64,32},{96,64},{33,1},{65,33},{97,65},{34,2},{66,34},{98,6... | collective-permute-start | bytes 786440 | tf_op jit(solution)/shard_map/ppermute | solution.py:27
  14.8 12.0 %collective-permute-start.3 = (bf16[10,1,128,128]{3,2,1,0:T(8,128)(2,1)S(1)}, bf16[10,1,128,128]{3,2,1,0:T(8,128)(2,1)S(1)}, u32[]{:S(2)}, u32[]{:S(2)}) collective-permute-start(bf16[10,1,128,128]{3,2,1,0:T(8,128)(2,1)S(1)} %pad_maximum_fusion.9), channel_id=1, source_target_pairs={{8,0},{16,8},{24,16},{9,1},{17,9},{25,17},{10,2},{18,10},{26,18},{... | collective-permute-start | bytes 983048 | tf_op jit(solution)/shard_map/ppermute | solution.py:27
  18.6 9.4 %collective-permute-start.2 = (bf16[10,1,128,128]{3,2,1,0:T(8,128)(2,1)S(1)}, bf16[10,1,128,128]{3,2,1,0:T(8,128)(2,1)S(1)}, u32[]{:S(2)}, u32[]{:S(2)}) collective-permute-start(bf16[10,1,128,128]{3,2,1,0:T(8,128)(2,1)S(1)} %pad_maximum_fusion.8), channel_id=1, source_target_pairs={{0,8},{8,16},{16,24},{1,9},{9,17},{17,25},{2,10},{10,18},{18,26},{... | collective-permute-start | bytes 983048 | tf_op jit(solution)/shard_map/ppermute | solution.py:27
  28.2 16.6 %collective-permute-start.5 = (bf16[10,10,32,128]{3,2,1,0:T(8,128)(2,1)S(1)}, bf16[10,10,32,128]{3,2,1,0:T(8,128)(2,1)S(1)}, u32[]{:S(2)}, u32[]{:S(2)}) collective-permute-start(bf16[10,10,32,128]{3,2,1,0:T(8,128)(2,1)S(1)} %pad_maximum_fusion.1), channel_id=1, source_target_pairs={{1,0},{2,1},{3,2},{4,3},{5,4},{6,5},{7,6},{9,8},{10,9},{11,10},{12... | collective-permute-start | bytes 2457608 | tf_op jit(solution)/shard_map/ppermute | solution.py:27
  29.6 17.0 %collective-permute-start.4 = (bf16[10,10,32,128]{3,2,1,0:T(8,128)(2,1)S(1)}, bf16[10,10,32,128]{3,2,1,0:T(8,128)(2,1)S(1)}, u32[]{:S(2)}, u32[]{:S(2)}) collective-permute-start(bf16[10,10,32,128]{3,2,1,0:T(8,128)(2,1)S(1)} %pad_maximum_fusion), channel_id=1, source_target_pairs={{0,1},{1,2},{2,3},{3,4},{4,5},{5,6},{6,7},{8,9},{9,10},{10,11},{11... | collective-permute-start | bytes 2457608 | tf_op jit(solution)/shard_map/ppermute | solution.py:27
  60.3 21.7 %all-to-all-start = ((bf16[32,64,128]{2,1,0:T(8,128)(2,1)}), bf16[32,64,128]{2,1,0:T(8,128)(2,1)S(1)}, u32[]{:S(2)}, u32[]{:S(2)}) async-start(bf16[32,64,128]{2,1,0:T(8,128)(2,1)} %copy.46), calls=%async_computation | async-start | bytes 1048576 | tf_op jit(solution)/shard_map/all_to_all | solution.py:417
  83.2 14.6 %copy-start.8 = (f32[4,128]{1,0:T(4,128)S(1)}, f32[4,128]{1,0:T(4,128)}, u32[]{:S(2)}) copy-start(f32[4,128]{1,0:T(4,128)} %param.11) | copy-start | bytes 6148
  83.2 29.7 %copy-start.9 = (f32[256,4]{0,1:T(4,128)S(1)}, f32[256,4]{0,1:T(4,128)}, u32[]{:S(2)}) copy-start(f32[256,4]{0,1:T(4,128)} %param.10) | copy-start | bytes 12292
  88.8 23.0 %all-to-all-start.1 = ((bf16[128,16,128]{2,1,0:T(8,128)(2,1)}), bf16[128,16,128]{2,1,0:T(8,128)(2,1)S(1)}, u32[]{:S(2)}, u32[]{:S(2)}) async-start(bf16[128,16,128]{2,1,0:T(8,128)(2,1)} %bitcast.200), calls=%async_computation.1 | async-start | bytes 1048576 | tf_op jit(solution)/shard_map/all_to_all | solution.py:417
  139.7 16.0 %all-to-all-start.3 = ((bf16[32,64,128]{2,1,0:T(8,128)(2,1)}), bf16[32,64,128]{2,1,0:T(8,128)(2,1)S(1)}, u32[]{:S(2)}, u32[]{:S(2)}) async-start(bf16[32,64,128]{2,1,0:T(8,128)(2,1)} %copy.50), calls=%async_computation.3 | async-start | bytes 1048576 | tf_op jit(solution)/shard_map/all_to_all | solution.py:417
  184.3 28.6 %collective-permute-start.6 = (bf16[10,192,128]{2,1,0:T(8,128)(2,1)}, bf16[10,192,128]{2,1,0:T(8,128)(2,1)S(1)}, u32[]{:S(2)}, u32[]{:S(2)}) collective-permute-start(bf16[10,192,128]{2,1,0:T(8,128)(2,1)} %get-tuple-element.43), channel_id=1, source_target_pairs={{0,32},{32,64},{64,96},{1,33},{33,65},{65,97},{2,34},{34,66},{66,9... | collective-permute-start | bytes 1474568 | tf_op jit(solution)/shard_map/ppermute | solution.py:27
  186.5 26.4 %collective-permute-start.7 = (bf16[10,192,128]{2,1,0:T(8,128)(2,1)}, bf16[10,192,128]{2,1,0:T(8,128)(2,1)S(1)}, u32[]{:S(2)}, u32[]{:S(2)}) collective-permute-start(bf16[10,192,128]{2,1,0:T(8,128)(2,1)} %get-tuple-element.42), channel_id=1, source_target_pairs={{32,0},{64,32},{96,64},{33,1},{65,33},{97,65},{34,2},{66,34},{98,6... | collective-permute-start | bytes 1474568 | tf_op jit(solution)/shard_map/ppermute | solution.py:27
  188.9 17.3 %all-to-all-start.4 = ((f32[128,4,128]{2,1,0:T(4,128)}), f32[128,4,128]{2,1,0:T(4,128)S(1)}, u32[]{:S(2)}, u32[]{:S(2)}) async-start(f32[128,4,128]{2,1,0:T(4,128)} %reshape.241), calls=%async_computation.4 | async-start | bytes 524288 | tf_op jit(solution)/shard_map/all_to_all | solution.py:417
  207.1 38.0 %all-to-all-start.5 = ((f32[128,4,128]{2,1,0:T(4,128)}), f32[128,4,128]{2,1,0:T(4,128)S(1)}, u32[]{:S(2)}, u32[]{:S(2)}) async-start(f32[128,4,128]{2,1,0:T(4,128)} %broadcast_in_dim.14), calls=%async_computation.5 | async-start | bytes 524288 | tf_op jit(solution)/shard_map/all_to_all | solution.py:417
  212.9 20.5 %copy-start.3 = (bf16[32,64,128]{2,0,1:T(8,128)(2,1)S(1)}, bf16[32,64,128]{2,0,1:T(8,128)(2,1)}, u32[]{:S(2)}) copy-start(bf16[32,64,128]{2,0,1:T(8,128)(2,1)} %copy-done.2) | copy-start | bytes 1572868
  212.9 20.5 %copy-start.6 = (bf16[128,2048,1,1,1,1,1]{1,0,2,3,4,5,6:T(8,128)(2,1)S(1)}, bf16[128,2048,1,1,1,1,1]{1,0,2,3,4,5,6:T(8,128)(2,1)}, u32[]{:S(2)}) copy-start(bf16[128,2048,1,1,1,1,1]{1,0,2,3,4,5,6:T(8,128)(2,1)} %reshape.266) | copy-start | bytes 1572868
  214.0 12.2 %collective-permute-start.9 = (bf16[8,192,128]{2,1,0:T(8,128)(2,1)S(1)}, bf16[8,192,128]{2,1,0:T(8,128)(2,1)S(1)}, u32[]{:S(2)}, u32[]{:S(2)}) collective-permute-start(bf16[8,192,128]{2,1,0:T(8,128)(2,1)S(1)} %pad_maximum_fusion.7), channel_id=1, source_target_pairs={{8,0},{16,8},{24,16},{9,1},{17,9},{25,17},{10,2},{18,10},{26,18},{... | collective-permute-start | bytes 1179656 | tf_op jit(solution)/shard_map/ppermute | solution.py:27
  217.0 9.2 %collective-permute-start.8 = (bf16[8,192,128]{2,1,0:T(8,128)(2,1)S(1)}, bf16[8,192,128]{2,1,0:T(8,128)(2,1)S(1)}, u32[]{:S(2)}, u32[]{:S(2)}) collective-permute-start(bf16[8,192,128]{2,1,0:T(8,128)(2,1)S(1)} %pad_maximum_fusion.6), channel_id=1, source_target_pairs={{0,8},{8,16},{16,24},{1,9},{9,17},{17,25},{2,10},{10,18},{18,26},{... | collective-permute-start | bytes 1179656 | tf_op jit(solution)/shard_map/ppermute | solution.py:27
  226.2 7.2 %copy-start.4 = (bf16[8,192,128]{2,1,0:T(8,128)(2,1)}, bf16[8,192,128]{2,1,0:T(8,128)(2,1)S(1)}, u32[]{:S(2)}) copy-start(bf16[8,192,128]{2,1,0:T(8,128)(2,1)S(1)} %collective-permute-done.9.y_hi) | copy-start | bytes 1179652
  227.2 21.8 %collective-permute-start.11 = (bf16[8,8,32,128]{3,2,1,0:T(8,128)(2,1)}, bf16[8,8,32,128]{3,2,1,0:T(8,128)(2,1)}, u32[]{:S(2)}, u32[]{:S(2)}) collective-permute-start(bf16[8,8,32,128]{3,2,1,0:T(8,128)(2,1)} %pad_maximum_fusion.5), channel_id=1, source_target_pairs={{1,0},{2,1},{3,2},{4,3},{5,4},{6,5},{7,6},{9,8},{10,9},{11,10},{12... | collective-permute-start | bytes 1572872 | tf_op jit(solution)/shard_map/ppermute | solution.py:27
  228.6 18.4 %collective-permute-start.10 = (bf16[8,8,32,128]{3,2,0,1:T(8,128)(2,1)S(1)}, bf16[8,8,32,128]{3,2,0,1:T(8,128)(2,1)}, u32[]{:S(2)}, u32[]{:S(2)}) collective-permute-start(bf16[8,8,32,128]{3,2,0,1:T(8,128)(2,1)S(1)} %pad_maximum_fusion.3), channel_id=1, source_target_pairs={{0,1},{1,2},{2,3},{3,4},{4,5},{5,6},{6,7},{8,9},{9,10},{10,11},{11... | collective-permute-start | bytes 1572872 | tf_op jit(solution)/shard_map/ppermute | solution.py:27
  (3 other events, 14.7 us)

commit v2 on v1

--- a/solution.py
+++ b/solution.py
@@ -208,7 +208,7 @@
 
         @pl.when(step == nx // 2 - 1)
         def _():
-            for dx in range(3):
+            def collect(dx, carry):
                 for dy in range(3):
                     for dz in range(3):
                         total = None
@@ -217,6 +217,9 @@
                             piece = sums[dx, start : start + c_in, z * c_out : (z + 1) * c_out]
                             total = piece if total is None else total + piece
                         result[9 * dx + 3 * dy + dz] = total
+                return carry
+
+            lax.fori_loop(0, 3, collect, 0)
 
     return pl.pallas_call(
         body,
@@ -246,7 +249,7 @@
     nx, ny, rows, lanes = grad_out.shape
     depth = matrix.shape[0]
 
-    def body(grad_out, matrix, spread, faces, held):
+    def body(grad_out, matrix, spread, x_first, x_last, held):
         step = pl.program_id(0)
 
         @pl.when(step == 0)
@@ -286,7 +289,11 @@
                 values = values.astype(bf16)
                 spread[x, y] = values[:, :lanes]
                 spread[x, y + 1] = values[:, lanes:]
-        faces[0] = jnp.where(step == 0, spread[0], spread[1])
+        x_last[...] = spread[1]
+
+        @pl.when(step == 0)
+        def _():
+            x_first[...] = spread[0]
 
     return pl.pallas_call(
         body,
@@ -297,11 +304,13 @@
         ],
         out_specs=[
             pl.BlockSpec((2, ny + 2, depth, lanes), lambda i: (i, 0, 0, 0)),
-            pl.BlockSpec((1, ny + 2, depth, lanes), lambda i: (jnp.minimum(i, 1), 0, 0, 0)),
+            pl.BlockSpec((ny + 2, depth, lanes), lambda i: (0, 0, 0)),
+            pl.BlockSpec((ny + 2, depth, lanes), lambda i: (0, 0, 0)),
         ],
         out_shape=[
             pltpu.HBM((nx + 2, ny + 2, depth, lanes), bf16),
-            jax.ShapeDtypeStruct((2, ny + 2, depth, lanes), bf16),
+            jax.ShapeDtypeStruct((ny + 2, depth, lanes), bf16),
+            jax.ShapeDtypeStruct((ny + 2, depth, lanes), bf16),
         ],
         scratch_shapes=[pltpu.VMEM((nx + 4, ny + 4, rows, lanes), bf16)],
         compiler_params=pltpu.CompilerParams(vmem_limit_bytes=40 * 2**20),
@@ -383,8 +392,8 @@
         x_hi,
         in_hbm(y_lo),
         in_hbm(y_hi),
-        in_hbm(z_lo),
-        in_hbm(z_hi),
+        z_lo,
+        z_hi,
     )
 
 
@@ -491,8 +500,8 @@
     ).reshape(pooled.shape)
 
     grad_out, kernel_local = kernel_grad_call(padded, conv_out, grad_pooled, c_in)
-    spread, x_faces = input_grad_call(grad_out, backward_matrix)
-    from_lo, from_hi = both_ways(x_faces[1], x_faces[0], "gx")
+    spread, x_first, x_last = input_grad_call(grad_out, backward_matrix)
+    from_lo, from_hi = both_ways(x_last, x_first, "gx")
 
     def added(array, first_term, last_term):
         head = (array[:1].astype(f32) + first_term.astype(f32)).astype(bf16)

time: 256 us -> 256 us (level)
  transfers between devices with their start and end apart: 17 -> 17, of which waited for: 11 -> 12; matrix products, arithmetic and copies ran while one was open for 16% -> 16% of each run, Pallas kernels for 1% -> 1%
where the time goes in v2:
time: 256 us; the launch traced here: 254 us
  starting transfers between devices  72.8 us (28%)
  waiting for transfers between devices  56.1 us (22%)
  Pallas kernels  50.8 us (20%)
  local copies, waits for them, and re-layouts  39.2 us (15%)
  blocking collectives  17.9 us (7%)
  matrix products  10 us (4%)
  other arithmetic  6.02 us (2%)
    all_to_all x5, starting transfers between devices, exchange(): return lax.all_to_all(array, axes, split_axis=0, concat_axis=0, tiled=True)  36 us
    all_to_all x5, waiting for transfers between devices, exchange(): return lax.all_to_all(array, axes, split_axis=0, concat_axis=0, tiled=True)  33 us
    ppermute x6, starting transfers between devices, both_ways(): lax.ppermute(toward_up, axis, up)  24.9 us
    ppermute x6, waiting for transfers between devices, both_ways(): lax.ppermute(toward_down, axis, down)  18.6 us
    all_to_all x1, blocking collectives, exchange(): return lax.all_to_all(array, axes, split_axis=0, concat_axis=0, tiled=True)  17.9 us
    pallas_call x1, Pallas kernels, input_grad_call(): pl.pallas_call(body, grid=(nx // 2 + 1,), in_specs=[pl.BlockSpec((2, ny,...  14.5 us
    pallas_call x1, Pallas kernels, forward_call(): pl.pallas_call(body, grid=(nx // 2,), in_specs=[whole(a) for a in operand...  12.5 us
    pallas_call x1, Pallas kernels, kernel_grad_call(): pl.pallas_call(body, grid=(nx // 2,), in_specs=[pl.BlockSpec((2,) + padde...  12.3 us
  transfers between devices with their start and end apart: 17, of which 12 were waited for; matrix products, arithmetic and copies ran while one was open for 16% of the time, Pallas kernels for 1%

profile of v2, /device:TPU:1, one launch (start us, length us, event | category | flops | bytes accessed | tf_op | source)
XLA Modules:
  0.0 254.0 jit_solution(4327710510069848456)
XLA Ops:
  1.9 4.0 %collective-permute-start = (bf16[1,8,128,128]{3,2,1,0:T(8,128)(2,1)S(1)}, bf16[1,8,128,128]{3,2,1,0:T(8,128)(2,1)S(1)}, u32[]{:S(2)}, u32[]{:S(2)}) collective-permute-start(bf16[1,8,128,128]{3,2,1,0:T(8,128)(2,1)S(1)} %bitcast.203), channel_id=1, source_target_pairs={{0,32},{32,64},{64,96},{1,33},{33,65},{65,97},{2,34},{34,66},{66,9... | collective-permute-start | bytes 786440 | tf_op jit(solution)/shard_map/ppermute | solution.py:27
  10.9 3.8 %collective-permute-done.1 = bf16[1,8,128,128]{3,2,1,0:T(8,128)(2,1)S(1)} collective-permute-done((bf16[1,8,128,128]{3,2,1,0:T(8,128)(2,1)S(1)}, bf16[1,8,128,128]{3,2,1,0:T(8,128)(2,1)S(1)}, u32[]{:S(2)}, u32[]{:S(2)}) %collective-permute-start.1) | collective-permute-done | bytes 262176 | tf_op jit(solution)/shard_map/ppermute | solution.py:27
  18.6 5.4 %collective-permute-start.2 = (bf16[10,1,128,128]{3,2,1,0:T(8,128)(2,1)S(1)}, bf16[10,1,128,128]{3,2,1,0:T(8,128)(2,1)S(1)}, u32[]{:S(2)}, u32[]{:S(2)}) collective-permute-start(bf16[10,1,128,128]{3,2,1,0:T(8,128)(2,1)S(1)} %pad_maximum_fusion.8), channel_id=1, source_target_pairs={{0,8},{8,16},{16,24},{1,9},{9,17},{17,25},{2,10},{10,18},{18,26},{... | collective-permute-start | bytes 983048 | tf_op jit(solution)/shard_map/ppermute | solution.py:27
  29.6 4.0 %collective-permute-start.4 = (bf16[10,10,32,128]{3,2,1,0:T(8,128)(2,1)S(1)}, bf16[10,10,32,128]{3,2,1,0:T(8,128)(2,1)S(1)}, u32[]{:S(2)}, u32[]{:S(2)}) collective-permute-start(bf16[10,10,32,128]{3,2,1,0:T(8,128)(2,1)S(1)} %pad_maximum_fusion), channel_id=1, source_target_pairs={{0,1},{1,2},{2,3},{3,4},{4,5},{5,6},{6,7},{8,9},{9,10},{10,11},{11... | collective-permute-start | bytes 2457608 | tf_op jit(solution)/shard_map/ppermute | solution.py:27
  35.3 9.4 %collective-permute-done.5.z_hi = bf16[10,10,32,128]{3,2,1,0:T(8,128)(2,1)S(1)} collective-permute-done((bf16[10,10,32,128]{3,2,1,0:T(8,128)(2,1)S(1)}, bf16[10,10,32,128]{3,2,1,0:T(8,128)(2,1)S(1)}, u32[]{:S(2)}, u32[]{:S(2)}) %collective-permute-start.5) | collective-permute-done | bytes 819232 | tf_op jit(solution)/shard_map/ppermute | solution.py:27
  46.6 12.5 %conv_forward.1 = (bf16[10,10,192,128]{3,2,1,0:T(8,128)(2,1)}, bf16[8,8,256,128]{3,2,1,0:T(8,128)(2,1)}, bf16[4,4,2,64,128]{4,3,2,1,0:T(8,128)(2,1)S(1)}) custom-call(bf16[8,8,128,128]{3,2,1,0:T(8,128)(2,1)} %bitcast.193, bf16[8,128,128]{2,1,0:T(8,128)(2,1)S(1)} %bitcast.180, bf16[8,128,128]{2,1,0:T(8,128)(2,1)S(1)} %bitcast.181, ...), custom_call_target="tpu_custom_call" | custom-call | flops 7000000000 | bytes 16777216 | tf_op jit(solution)/shard_map/conv_forward/pallas_call | solution.py:148
  60.3 10.2 %all-to-all-start = ((bf16[32,64,128]{2,1,0:T(8,128)(2,1)}), bf16[32,64,128]{2,1,0:T(8,128)(2,1)S(1)}, u32[]{:S(2)}, u32[]{:S(2)}) async-start(bf16[32,64,128]{2,1,0:T(8,128)(2,1)} %copy.46), calls=%async_computation | async-start | bytes 1048576 | tf_op jit(solution)/shard_map/all_to_all | solution.py:426
  70.5 11.4 %copy.44 = bf16[4,16,2,16,2048]{4,3,2,1,0:T(8,128)(2,1)} copy(bf16[4,16,2,16,2048]{4,2,3,1,0:T(2,128)(2,1)} %bitcast.186) | data formatting | bytes 16777216 | tf_op jit(solution)/shard_map/transpose | solution.py:464
  83.2 4.7 %fusion.1 = bf16[16,8,16,128]{3,1,2,0:T(8,128)(2,1)S(1)} fusion(bf16[2048,128]{1,0:T(8,128)(2,1)S(1)} %bitcast.189, bf16[2048,2048]{1,0:T(8,128)(2,1)} %bitcast.184), kind=kOutput, calls=%fused_computation.3 | convolution fusion | flops 1074003968 | bytes 9437184 | tf_op jit(solution)/shard_map/dot_general | solution.py:466
  88.8 9.0 %all-to-all-start.1 = ((bf16[128,16,128]{2,1,0:T(8,128)(2,1)}), bf16[128,16,128]{2,1,0:T(8,128)(2,1)S(1)}, u32[]{:S(2)}, u32[]{:S(2)}) async-start(bf16[128,16,128]{2,1,0:T(8,128)(2,1)} %bitcast.196), calls=%async_computation.1 | async-start | bytes 1048576 | tf_op jit(solution)/shard_map/all_to_all | solution.py:426
  98.0 13.8 %all-to-all-done.1 = bf16[128,16,128]{2,1,0:T(8,128)(2,1)S(1)} async-done(((bf16[128,16,128]{2,1,0:T(8,128)(2,1)}), bf16[128,16,128]{2,1,0:T(8,128)(2,1)S(1)}, u32[]{:S(2)}, u32[]{:S(2)}) %all-to-all-start.1) | async-done | bytes 524320 | tf_op jit(solution)/shard_map/all_to_all | solution.py:426
  115.1 17.9 %all_to_all.30 = bf16[128,16,128]{2,1,0:T(8,128)(2,1)S(1)} all-to-all(bf16[128,16,128]{2,1,0:T(8,128)(2,1)S(1)} %broadcast_in_dim.11), channel_id=1, replica_groups=mesh['gx'=4,'gy'=4,'gz'=8] {'gx','gy','gz'}, dimensions={0} | all-to-all | bytes 1048576 | tf_op jit(solution)/shard_map/all_to_all | solution.py:426
  133.1 5.5 %feature_grad.1 = bf16[2048,128]{1,0:T(8,128)(2,1)S(1)} custom-call(bf16[2048,2048]{1,0:T(8,128)(2,1)} %bitcast.185, bf16[128,2048]{1,0:T(8,128)(2,1)S(1)} %bitcast.177), custom_call_target="tpu_custom_call" | custom-call | flops 1000000000 | bytes 10485760 | tf_op jit(solution)/shard_map/feature_grad/pallas_call | solution.py:410
  139.7 4.4 %all-to-all-start.3 = ((bf16[32,64,128]{2,1,0:T(8,128)(2,1)}), bf16[32,64,128]{2,1,0:T(8,128)(2,1)S(1)}, u32[]{:S(2)}, u32[]{:S(2)}) async-start(bf16[32,64,128]{2,1,0:T(8,128)(2,1)} %copy.50), calls=%async_computation.3 | async-start | bytes 1048576 | tf_op jit(solution)/shard_map/all_to_all | solution.py:426
  145.2 10.6 %all-to-all-done.3 = bf16[32,64,128]{2,1,0:T(8,128)(2,1)S(1)} async-done(((bf16[32,64,128]{2,1,0:T(8,128)(2,1)}), bf16[32,64,128]{2,1,0:T(8,128)(2,1)S(1)}, u32[]{:S(2)}, u32[]{:S(2)}) %all-to-all-start.3) | async-done | bytes 524320 | tf_op jit(solution)/shard_map/all_to_all | solution.py:426
  156.6 12.3 %conv_kernel_grad.1 = (bf16[8,8,256,128]{3,2,1,0:T(8,128)(2,1)}, f32[27,32,64]{2,1,0:T(8,128)S(1)}) custom-call(bf16[10,10,192,128]{3,2,1,0:T(8,128)(2,1)} %get-tuple-element.15.rows_0.rows_1, bf16[10,10,192,128]{3,2,1,0:T(8,128)(2,1)} %get-tuple-element.15.rows_0.rows_1, bf16[8,8,256,128]{3,2,1,0:T(8,128)(2,1)} %get-tuple-element.16.conv_out, ...), custom_call_target="tpu_custom_call" | custom-call | flops 8000000000 | bytes 14680064 | tf_op jit(solution)/shard_map/conv_kernel_grad/pallas_call | solution.py:224
  168.9 14.5 %conv_input_grad.1 = (bf16[10,10,192,128]{3,2,1,0:T(8,128)(2,1)}, bf16[10,192,128]{2,1,0:T(8,128)(2,1)S(1)}, bf16[10,192,128]{2,1,0:T(8,128)(2,1)S(1)}) custom-call(bf16[8,8,256,128]{3,2,1,0:T(8,128)(2,1)} %get-tuple-element.19.grad_out, bf16[192,2304]{1,0:T(8,128)(2,1)S(1)} %get-tuple-element.20.matrix), custom_call_target="tpu_custom_call" | custom-call | flops 8999999488 | bytes 12582912 | tf_op jit(solution)/shard_map/conv_input_grad/pallas_call | solution.py:298
  188.1 6.5 %all-to-all-start.4 = ((f32[128,4,128]{2,1,0:T(4,128)}), f32[128,4,128]{2,1,0:T(4,128)}, u32[]{:S(2)}, u32[]{:S(2)}) async-start(f32[128,4,128]{2,1,0:T(4,128)} %reshape.241), calls=%async_computation.4 | async-start | bytes 524288 | tf_op jit(solution)/shard_map/all_to_all | solution.py:426
  196.8 8.6 %all-to-all-done.4 = f32[128,4,128]{2,1,0:T(4,128)} async-done(((f32[128,4,128]{2,1,0:T(4,128)}), f32[128,4,128]{2,1,0:T(4,128)}, u32[]{:S(2)}, u32[]{:S(2)}) %all-to-all-start.4) | async-done | bytes 262176 | tf_op jit(solution)/shard_map/all_to_all | solution.py:426
  207.3 6.0 %all-to-all-start.5 = ((f32[128,4,128]{2,1,0:T(4,128)}), f32[128,4,128]{2,1,0:T(4,128)}, u32[]{:S(2)}, u32[]{:S(2)}) async-start(f32[128,4,128]{2,1,0:T(4,128)} %broadcast_in_dim.14), calls=%async_computation.5 | async-start | bytes 524288 | tf_op jit(solution)/shard_map/all_to_all | solution.py:426
  217.6 4.3 %collective-permute-start.8 = (bf16[8,192,128]{2,1,0:T(8,128)(2,1)S(1)}, bf16[8,192,128]{2,1,0:T(8,128)(2,1)S(1)}, u32[]{:S(2)}, u32[]{:S(2)}) collective-permute-start(bf16[8,192,128]{2,1,0:T(8,128)(2,1)S(1)} %pad_maximum_fusion.6), channel_id=1, source_target_pairs={{0,8},{8,16},{16,24},{1,9},{9,17},{17,25},{2,10},{10,18},{18,26},{... | collective-permute-start | bytes 1179656 | tf_op jit(solution)/shard_map/ppermute | solution.py:27
  228.9 4.8 %collective-permute-start.10 = (bf16[8,8,32,128]{3,2,0,1:T(8,128)(2,1)S(1)}, bf16[8,8,32,128]{3,2,0,1:T(8,128)(2,1)}, u32[]{:S(2)}, u32[]{:S(2)}) collective-permute-start(bf16[8,8,32,128]{3,2,0,1:T(8,128)(2,1)S(1)} %pad_maximum_fusion.3), channel_id=1, source_target_pairs={{0,1},{1,2},{2,3},{3,4},{4,5},{5,6},{6,7},{8,9},{9,10},{10,11},{11... | collective-permute-start | bytes 1572872 | tf_op jit(solution)/shard_map/ppermute | solution.py:27
  236.0 9.4 %copy.55 = bf16[4,4,4,8,2,2,2048]{6,5,4,3,2,1,0:T(2,128)(2,1)} copy(bf16[4,4,4,8,2,2,2048]{6,3,5,4,2,0,1:T(8,128)(2,1)S(1)} %fusion) | data formatting | bytes 16777216 | tf_op jit(solution)/shard_map/convert_element_type | solution.py:497
  249.5 4.5 %fold_faces.1 = bf16[8,8,128,128]{3,2,1,0:T(8,128)(2,1)} custom-call(bf16[10,10,192,128]{3,2,1,0:T(8,128)(2,1)} %get-tuple-element.21.spread_0.spread_1, bf16[10,10,192,128]{3,2,1,0:T(8,128)(2,1)} %get-tuple-element.21.spread_0.spread_1, bf16[10,192,128]{2,1,0:T(8,128)(2,1)S(1)} %collective-permute-done.6.x_lo, ...), custom_call_target="tpu_custom_call" | custom-call | flops 100000000 | bytes 10485760 | tf_op jit(solution)/shard_map/fold_faces/pallas_call | solution.py:370
  (104 shorter events, 55.4 us)
Async XLA Ops:
  0.6 111.3 %copy-start = (f32[2048,256]{1,0:T(8,128)S(1)}, f32[2048,256]{1,0:T(8,128)}, u32[]{:S(2)}) copy-start(f32[2048,256]{1,0:T(8,128)} %param.9) | copy-start | bytes 6291460
  0.6 33.0 %copy-start.7 = (bf16[3,3,3,32,64]{4,3,2,1,0:T(8,128)(2,1)S(1)}, bf16[3,3,3,32,64]{4,3,2,1,0:T(8,128)(2,1)}, u32[]{:S(2)}) copy-start(bf16[3,3,3,32,64]{4,3,2,1,0:T(8,128)(2,1)} %param.7) | copy-start | bytes 331780
  1.9 9.0 %collective-permute-start = (bf16[1,8,128,128]{3,2,1,0:T(8,128)(2,1)S(1)}, bf16[1,8,128,128]{3,2,1,0:T(8,128)(2,1)S(1)}, u32[]{:S(2)}, u32[]{:S(2)}) collective-permute-start(bf16[1,8,128,128]{3,2,1,0:T(8,128)(2,1)S(1)} %bitcast.203), channel_id=1, source_target_pairs={{0,32},{32,64},{64,96},{1,33},{33,65},{65,97},{2,34},{34,66},{66,9... | collective-permute-start | bytes 786440 | tf_op jit(solution)/shard_map/ppermute | solution.py:27
  5.9 8.8 %collective-permute-start.1 = (bf16[1,8,128,128]{3,2,1,0:T(8,128)(2,1)S(1)}, bf16[1,8,128,128]{3,2,1,0:T(8,128)(2,1)S(1)}, u32[]{:S(2)}, u32[]{:S(2)}) collective-permute-start(bf16[1,8,128,128]{3,2,1,0:T(8,128)(2,1)S(1)} %bitcast.202), channel_id=1, source_target_pairs={{32,0},{64,32},{96,64},{33,1},{65,33},{97,65},{34,2},{66,34},{98,6... | collective-permute-start | bytes 786440 | tf_op jit(solution)/shard_map/ppermute | solution.py:27
  14.8 12.0 %collective-permute-start.3 = (bf16[10,1,128,128]{3,2,1,0:T(8,128)(2,1)S(1)}, bf16[10,1,128,128]{3,2,1,0:T(8,128)(2,1)S(1)}, u32[]{:S(2)}, u32[]{:S(2)}) collective-permute-start(bf16[10,1,128,128]{3,2,1,0:T(8,128)(2,1)S(1)} %pad_maximum_fusion.9), channel_id=1, source_target_pairs={{8,0},{16,8},{24,16},{9,1},{17,9},{25,17},{10,2},{18,10},{26,18},{... | collective-permute-start | bytes 983048 | tf_op jit(solution)/shard_map/ppermute | solution.py:27
  18.6 9.4 %collective-permute-start.2 = (bf16[10,1,128,128]{3,2,1,0:T(8,128)(2,1)S(1)}, bf16[10,1,128,128]{3,2,1,0:T(8,128)(2,1)S(1)}, u32[]{:S(2)}, u32[]{:S(2)}) collective-permute-start(bf16[10,1,128,128]{3,2,1,0:T(8,128)(2,1)S(1)} %pad_maximum_fusion.8), channel_id=1, source_target_pairs={{0,8},{8,16},{16,24},{1,9},{9,17},{17,25},{2,10},{10,18},{18,26},{... | collective-permute-start | bytes 983048 | tf_op jit(solution)/shard_map/ppermute | solution.py:27
  28.2 16.6 %collective-permute-start.5 = (bf16[10,10,32,128]{3,2,1,0:T(8,128)(2,1)S(1)}, bf16[10,10,32,128]{3,2,1,0:T(8,128)(2,1)S(1)}, u32[]{:S(2)}, u32[]{:S(2)}) collective-permute-start(bf16[10,10,32,128]{3,2,1,0:T(8,128)(2,1)S(1)} %pad_maximum_fusion.1), channel_id=1, source_target_pairs={{1,0},{2,1},{3,2},{4,3},{5,4},{6,5},{7,6},{9,8},{10,9},{11,10},{12... | collective-permute-start | bytes 2457608 | tf_op jit(solution)/shard_map/ppermute | solution.py:27
  29.6 17.0 %collective-permute-start.4 = (bf16[10,10,32,128]{3,2,1,0:T(8,128)(2,1)S(1)}, bf16[10,10,32,128]{3,2,1,0:T(8,128)(2,1)S(1)}, u32[]{:S(2)}, u32[]{:S(2)}) collective-permute-start(bf16[10,10,32,128]{3,2,1,0:T(8,128)(2,1)S(1)} %pad_maximum_fusion), channel_id=1, source_target_pairs={{0,1},{1,2},{2,3},{3,4},{4,5},{5,6},{6,7},{8,9},{9,10},{10,11},{11... | collective-permute-start | bytes 2457608 | tf_op jit(solution)/shard_map/ppermute | solution.py:27
  60.3 21.7 %all-to-all-start = ((bf16[32,64,128]{2,1,0:T(8,128)(2,1)}), bf16[32,64,128]{2,1,0:T(8,128)(2,1)S(1)}, u32[]{:S(2)}, u32[]{:S(2)}) async-start(bf16[32,64,128]{2,1,0:T(8,128)(2,1)} %copy.46), calls=%async_computation | async-start | bytes 1048576 | tf_op jit(solution)/shard_map/all_to_all | solution.py:426
  83.2 14.6 %copy-start.8 = (f32[4,128]{1,0:T(4,128)S(1)}, f32[4,128]{1,0:T(4,128)}, u32[]{:S(2)}) copy-start(f32[4,128]{1,0:T(4,128)} %param.11) | copy-start | bytes 6148
  83.2 29.7 %copy-start.9 = (f32[256,4]{0,1:T(4,128)S(1)}, f32[256,4]{0,1:T(4,128)}, u32[]{:S(2)}) copy-start(f32[256,4]{0,1:T(4,128)} %param.10) | copy-start | bytes 12292
  88.8 22.9 %all-to-all-start.1 = ((bf16[128,16,128]{2,1,0:T(8,128)(2,1)}), bf16[128,16,128]{2,1,0:T(8,128)(2,1)S(1)}, u32[]{:S(2)}, u32[]{:S(2)}) async-start(bf16[128,16,128]{2,1,0:T(8,128)(2,1)} %bitcast.196), calls=%async_computation.1 | async-start | bytes 1048576 | tf_op jit(solution)/shard_map/all_to_all | solution.py:426
  139.7 16.0 %all-to-all-start.3 = ((bf16[32,64,128]{2,1,0:T(8,128)(2,1)}), bf16[32,64,128]{2,1,0:T(8,128)(2,1)S(1)}, u32[]{:S(2)}, u32[]{:S(2)}) async-start(bf16[32,64,128]{2,1,0:T(8,128)(2,1)} %copy.50), calls=%async_computation.3 | async-start | bytes 1048576 | tf_op jit(solution)/shard_map/all_to_all | solution.py:426
  183.4 30.0 %collective-permute-start.6 = (bf16[10,192,128]{2,1,0:T(8,128)(2,1)S(1)}, bf16[10,192,128]{2,1,0:T(8,128)(2,1)S(1)}, u32[]{:S(2)}, u32[]{:S(2)}) collective-permute-start(bf16[10,192,128]{2,1,0:T(8,128)(2,1)S(1)} %get-tuple-element.22), channel_id=1, source_target_pairs={{0,32},{32,64},{64,96},{1,33},{33,65},{65,97},{2,34},{34,66},{66,9... | collective-permute-start | bytes 1474568 | tf_op jit(solution)/shard_map/ppermute | solution.py:27
  185.7 27.7 %collective-permute-start.7 = (bf16[10,192,128]{2,1,0:T(8,128)(2,1)S(1)}, bf16[10,192,128]{2,1,0:T(8,128)(2,1)S(1)}, u32[]{:S(2)}, u32[]{:S(2)}) collective-permute-start(bf16[10,192,128]{2,1,0:T(8,128)(2,1)S(1)} %get-tuple-element.23), channel_id=1, source_target_pairs={{32,0},{64,32},{96,64},{33,1},{65,33},{97,65},{34,2},{66,34},{98,6... | collective-permute-start | bytes 1474568 | tf_op jit(solution)/shard_map/ppermute | solution.py:27
  188.1 17.3 %all-to-all-start.4 = ((f32[128,4,128]{2,1,0:T(4,128)}), f32[128,4,128]{2,1,0:T(4,128)}, u32[]{:S(2)}, u32[]{:S(2)}) async-start(f32[128,4,128]{2,1,0:T(4,128)} %reshape.241), calls=%async_computation.4 | async-start | bytes 524288 | tf_op jit(solution)/shard_map/all_to_all | solution.py:426
  207.3 38.1 %all-to-all-start.5 = ((f32[128,4,128]{2,1,0:T(4,128)}), f32[128,4,128]{2,1,0:T(4,128)}, u32[]{:S(2)}, u32[]{:S(2)}) async-start(f32[128,4,128]{2,1,0:T(4,128)} %broadcast_in_dim.14), calls=%async_computation.5 | async-start | bytes 524288 | tf_op jit(solution)/shard_map/all_to_all | solution.py:426
  213.3 20.4 %copy-start.3 = (bf16[32,64,128]{2,0,1:T(8,128)(2,1)S(1)}, bf16[32,64,128]{2,0,1:T(8,128)(2,1)}, u32[]{:S(2)}) copy-start(bf16[32,64,128]{2,0,1:T(8,128)(2,1)} %copy-done.2) | copy-start | bytes 1572868
  213.3 20.4 %copy-start.6 = (bf16[128,2048,1,1,1,1,1]{1,0,2,3,4,5,6:T(8,128)(2,1)S(1)}, bf16[128,2048,1,1,1,1,1]{1,0,2,3,4,5,6:T(8,128)(2,1)}, u32[]{:S(2)}) copy-start(bf16[128,2048,1,1,1,1,1]{1,0,2,3,4,5,6:T(8,128)(2,1)} %reshape.266) | copy-start | bytes 1572868
  214.4 12.0 %collective-permute-start.9 = (bf16[8,192,128]{2,1,0:T(8,128)(2,1)S(1)}, bf16[8,192,128]{2,1,0:T(8,128)(2,1)S(1)}, u32[]{:S(2)}, u32[]{:S(2)}) collective-permute-start(bf16[8,192,128]{2,1,0:T(8,128)(2,1)S(1)} %pad_maximum_fusion.7), channel_id=1, source_target_pairs={{8,0},{16,8},{24,16},{9,1},{17,9},{25,17},{10,2},{18,10},{26,18},{... | collective-permute-start | bytes 1179656 | tf_op jit(solution)/shard_map/ppermute | solution.py:27
  217.6 9.0 %collective-permute-start.8 = (bf16[8,192,128]{2,1,0:T(8,128)(2,1)S(1)}, bf16[8,192,128]{2,1,0:T(8,128)(2,1)S(1)}, u32[]{:S(2)}, u32[]{:S(2)}) collective-permute-start(bf16[8,192,128]{2,1,0:T(8,128)(2,1)S(1)} %pad_maximum_fusion.6), channel_id=1, source_target_pairs={{0,8},{8,16},{16,24},{1,9},{9,17},{17,25},{2,10},{10,18},{18,26},{... | collective-permute-start | bytes 1179656 | tf_op jit(solution)/shard_map/ppermute | solution.py:27
  226.5 9.6 %copy-start.4 = (bf16[8,192,128]{2,1,0:T(8,128)(2,1)}, bf16[8,192,128]{2,1,0:T(8,128)(2,1)S(1)}, u32[]{:S(2)}) copy-start(bf16[8,192,128]{2,1,0:T(8,128)(2,1)S(1)} %collective-permute-done.9.y_hi) | copy-start | bytes 1179652
  227.5 22.0 %collective-permute-start.11 = (bf16[8,8,32,128]{3,2,1,0:T(8,128)(2,1)}, bf16[8,8,32,128]{3,2,1,0:T(8,128)(2,1)}, u32[]{:S(2)}, u32[]{:S(2)}) collective-permute-start(bf16[8,8,32,128]{3,2,1,0:T(8,128)(2,1)} %pad_maximum_fusion.5), channel_id=1, source_target_pairs={{1,0},{2,1},{3,2},{4,3},{5,4},{6,5},{7,6},{9,8},{10,9},{11,10},{12... | collective-permute-start | bytes 1572872 | tf_op jit(solution)/shard_map/ppermute | solution.py:27
  228.9 19.4 %collective-permute-start.10 = (bf16[8,8,32,128]{3,2,0,1:T(8,128)(2,1)S(1)}, bf16[8,8,32,128]{3,2,0,1:T(8,128)(2,1)}, u32[]{:S(2)}, u32[]{:S(2)}) collective-permute-start(bf16[8,8,32,128]{3,2,0,1:T(8,128)(2,1)S(1)} %pad_maximum_fusion.3), channel_id=1, source_target_pairs={{0,1},{1,2},{2,3},{3,4},{4,5},{5,6},{6,7},{8,9},{9,10},{10,11},{11... | collective-permute-start | bytes 1572872 | tf_op jit(solution)/shard_map/ppermute | solution.py:27
  (3 other events, 16.1 us)
